TPU v7x, 8 devices: a whole 2x2x1 slice. The times are simulated.
8 devices in a mesh: dp: 1 (over z), ep: 8 (over y, x, core).
Axes of the slice: x: 2, y: 2, z: 1, core: 2. Of those that a mesh axis runs over, the one named last changes fastest.
Arguments:
- tokens: bfloat16 [24576, 1024], P(('dp', 'ep'))
- expert_idx: int32 [24576], P(('dp', 'ep'))
- w_router: float32 [1024, 128], replicated
- w_in: bfloat16 [128, 1024, 2816], P('ep')
- w_out: bfloat16 [128, 2816, 1024], P('ep')
Outputs:
- output: bfloat16 [24576, 1024], P(('dp', 'ep'))
All inputs are finite; a program needn't handle non-finite values.
Results may differ from a plain program's by a relative error of at most 0.00104.
Values are sent between devices in bfloat16 or wider.
A program may use at most 1 GiB of HBM per device.

v0:
```python
import jax
import jax.numpy as jnp
from jax import lax
from jax.sharding import PartitionSpec as P, NamedSharding


def dispatch(tok_rows, choice, w_router, capacity):
    tok_count = tok_rows.shape[0]
    num_experts = w_router.shape[1]
    logits = jnp.dot(tok_rows.astype(jnp.float32), w_router, precision=lax.Precision.HIGHEST)
    router_prob = jax.nn.softmax(logits, axis=-1)
    chosen = choice[:, None] == jnp.arange(num_experts, dtype=jnp.int32)[None, :]
    gate_prob = jnp.sum(jnp.where(chosen, router_prob, 0.0), axis=-1)
    running_count = jnp.cumsum(chosen.astype(jnp.int32), axis=0) - 1
    position = jnp.sum(jnp.where(chosen, running_count, 0), axis=-1)
    slot_index = jnp.where(position < capacity, choice * capacity + position, num_experts * capacity)
    holder = jnp.full((num_experts * capacity + 1,), tok_count, jnp.int32).at[slot_index].set(jnp.arange(tok_count, dtype=jnp.int32))
    buffer = jnp.take(tok_rows, holder[:-1], axis=0, mode="fill", fill_value=0)
    return buffer, slot_index, gate_prob


def combine(flat_out, slot_index, gate_prob):
    picked = jnp.take(flat_out, slot_index, axis=0, mode="fill", fill_value=0)
    return (gate_prob[:, None] * picked.astype(jnp.float32)).astype(jnp.bfloat16)


def solution(mesh):
    groups = mesh.shape["ep"]

    def local_block(tokens, expert_idx, w_router, w_in, w_out):
        tok_count, model_dim = tokens.shape
        local_experts = w_in.shape[0]
        num_experts = local_experts * groups
        capacity = (5 * tok_count + 4 * num_experts - 1) // (4 * num_experts)
        buffer, slot_index, gate_prob = dispatch(tokens, expert_idx, w_router, capacity)
        send_buf = buffer.reshape(groups, local_experts, capacity, model_dim)
        recv_buf = lax.all_to_all(send_buf, "ep", 0, 2, tiled=True)
        rows_in = recv_buf.reshape(local_experts, groups * capacity, model_dim)
        hidden = jnp.einsum("ecd,edf->ecf", rows_in, w_in, preferred_element_type=jnp.float32)
        hidden_act = jax.nn.relu(hidden).astype(jnp.bfloat16)
        expert_rows = jnp.einsum("ecf,efd->ecd", hidden_act, w_out, preferred_element_type=jnp.float32).astype(jnp.bfloat16)
        back_buf = lax.all_to_all(expert_rows.reshape(1, local_experts, groups * capacity, model_dim), "ep", 2, 0, tiled=True)
        flat_out = back_buf.reshape(num_experts * capacity, model_dim)
        return combine(flat_out, slot_index, gate_prob)

    return jax.shard_map(local_block, mesh=mesh, in_specs=(P(("dp", "ep"), None), P(("dp", "ep")), P(None, None), P("ep", None, None), P("ep", None, None)), out_specs=P(("dp", "ep"), None), check_vma=False)
```

profile of v0, /device:TPU:0, one launch (start us, length us, event | category | flops | bytes accessed | tf_op | source)
XLA Modules:
  0.0 421.4 jit_solution(7243448520027020108)
XLA Ops:
  0.0 0.0 copy-start
  0.0 0.0 copy-start.1
  0.0 0.9 copy.13
  0.9 0.5 fusion.3
  1.4 1.3 add_add_fusion
  2.7 2.0 copy.14
  4.6 0.0 copy-done.1
  4.7 0.3 fusion.2
  5.0 11.8 %scatter_custom_fusion = s32[3841]{0:T(1024)S(1)} fusion(s32[3072]{0:T(1024)S(1)} %get-tuple-element.6, s32[3072]{0:T(1024)S(1)} %iota.11, s32[]{:T(128)} %constant.31.clone.1), kind=kCustom, calls=%fused_computation.30 | custom fusion | bytes 15368 | tf_op jit(solution)/shard_map/scatter | solution.py:17
  16.8 21.0 %gather_fusion = bf16[3840,1024]{1,0:T(8,128)(2,1)} fusion(bf16[3072,1024]{1,0:T(8,128)(2,1)} %param.5, s32[4096]{0:T(1024)S(1)} %pad_clamp_fusion), kind=kCustom, calls=%fused_computation | custom fusion | bytes 15744000 | tf_op jit(solution)/shard_map/jit(_take)/gather | solution.py:18
  37.9 11.3 %gather.11 = bf16[8,16,30,1024]{3,2,1,0:T(8,128)(2,1)} reshape(bf16[3840,1024]{1,0:T(8,128)(2,1)} %gather_fusion) | data formatting | bytes 15728640 | tf_op jit(solution)/shard_map/jit(_take)/gather | solution.py:18
  49.2 0.1 slice.14
  49.4 7.2 %broadcast_select_fusion = bf16[8,16,30,1024]{3,2,1,0:T(8,128)(2,1)} fusion(bf16[8,16,30,1024]{3,2,1,0:T(8,128)(2,1)} %gather.11, pred[8,16,30]{2,1,0:T(8,128)(4,1)S(1)} %compare_and_fusion), kind=kLoop, calls=%fused_computation.5 | loop fusion | flops 3932160 | bytes 15732480 | tf_op jit(solution)/shard_map/jit(_take)/select_n | solution.py:18
  56.6 11.5 %copy.15 = bf16[8,16,30,1024]{3,1,2,0:T(8,128)(2,1)} copy(bf16[8,16,30,1024]{3,2,1,0:T(8,128)(2,1)} %broadcast_select_fusion) | data formatting | bytes 15728640 | tf_op jit(solution)/shard_map/jit(_take)/select_n | solution.py:18
  68.1 93.7 %all_to_all.30 = bf16[8,16,30,1024]{3,1,2,0:T(8,128)(2,1)} all-to-all(bf16[8,16,30,1024]{3,1,2,0:T(8,128)(2,1)} %copy.15), channel_id=1, replica_groups=mesh['dp'=1,'ep'=8] {'ep'}, dimensions={0} | all-to-all | bytes 15728640 | tf_op jit(solution)/shard_map/all_to_all | solution.py:37
  161.8 64.7 %maximum_convert_fusion.clone.4 = bf16[16,240,2816]{2,1,0:T(8,128)(2,1)} fusion(bf16[16,1024,2816]{2,1,0:T(8,128)(2,1)} %param.8, bf16[16,240,1024]{2,0,1:T(8,128)(2,1)} %bitcast.38), kind=kOutput, calls=%fused_computation.3.clone.clone.clone.1 | convolution fusion | flops 22167552000 | bytes 121765888 | tf_op jit(solution)/shard_map/ecd,edf->ecf/dot_general | solution.py:39
  226.5 42.0 %convert_bitcast_fusion = bf16[1,16,240,1024]{3,2,1,0:T(8,128)(2,1)} fusion(bf16[16,2816,1024]{2,1,0:T(8,128)(2,1)} %param.9, bf16[16,240,2816]{2,1,0:T(8,128)(2,1)} %maximum_convert_fusion.clone.4), kind=kOutput, calls=%fused_computation.7 | convolution fusion | flops 22149857280 | bytes 121765888 | tf_op jit(solution)/shard_map/ecf,efd->ecd/dot_general | solution.py:41
  268.5 10.7 %copy.17 = bf16[1,16,240,1024]{3,1,0,2:T(8,128)(2,1)} copy(bf16[1,16,240,1024]{3,2,1,0:T(8,128)(2,1)} %convert_bitcast_fusion) | data formatting | bytes 15728640 | tf_op jit(solution)/shard_map/reshape | solution.py:42
  279.2 3.9 all-to-all-start.1
  283.2 0.0 copy-done
  283.2 8.3 %fusion.14 = (f32[3072]{0:T(1024)S(1)}, f32[3072,128]{0,1:T(8,128)S(1)}) fusion(bf16[3072,1024]{1,0:T(8,128)(2,1)} %param.5, f32[1024,128]{1,0:T(8,128)S(1)} %copy-done), kind=kOutput, calls=%fused_computation.34 | convolution fusion | flops 4832228352 | bytes 8400896 | tf_op jit(solution)/shard_map/dot_general | solution.py:10
  291.5 0.2 fusion.5
  291.8 0.4 select_reduce_fusion
  292.2 79.1 %all-to-all-done.1 = bf16[1,16,240,1024]{3,1,0,2:T(8,128)(2,1)} async-done(((bf16[1,16,240,1024]{3,1,0,2:T(8,128)(2,1)}), bf16[1,16,240,1024]{3,1,0,2:T(8,128)(2,1)}, u32[]{:S(2)}, u32[]{:S(2)}) %all-to-all-start.1) | async-done | bytes 7864352 | tf_op jit(solution)/shard_map/all_to_all | solution.py:42
  371.3 11.6 %copy.18 = bf16[8,1,16,30,1024]{4,3,2,0,1:T(8,128)(2,1)} copy(bf16[8,1,16,30,1024]{4,2,3,0,1:T(8,128)(2,1)} %bitcast.8) | data formatting | bytes 15728640 | tf_op jit(solution)/shard_map/all_to_all | solution.py:42
  382.9 11.2 %reshape.53 = bf16[3840,1024]{1,0:T(8,128)(2,1)} reshape(bf16[8,1,16,30,1024]{4,3,2,0,1:T(8,128)(2,1)} %copy.18) | data formatting | bytes 15728640 | tf_op jit(solution)/shard_map/reshape | solution.py:43
  394.1 20.1 %gather_fusion.1 = bf16[3072,1024]{1,0:T(8,128)(2,1)} fusion(bf16[3840,1024]{1,0:T(8,128)(2,1)} %reshape.53, s32[3072]{0:T(1024)S(1)} %get-tuple-element.5), kind=kCustom, calls=%fused_computation.1 | custom fusion | bytes 12595200 | tf_op jit(solution)/shard_map/jit(_take)/gather | solution.py:23
  414.2 7.2 %multiply_convert_fusion = bf16[3072,1024]{1,0:T(8,128)(2,1)} fusion(bf16[3072,1024]{1,0:T(8,128)(2,1)} %gather_fusion.1, f32[3072]{0:T(1024)S(1)} %select_reduce_fusion, pred[3072]{0:T(1024)(128)(4,1)S(1)} %compare_and_fusion.1), kind=kLoop, calls=%fused_computation.4 | loop fusion | flops 12582912 | bytes 12598272 | tf_op jit(solution)/shard_map/convert_element_type | solution.py:24
  (9 shorter events, 0.1 us)
Async XLA Ops:
  0.0 283.2 %copy-start = (f32[1024,128]{1,0:T(8,128)S(1)}, f32[1024,128]{1,0:T(8,128)}, u32[]{:S(2)}) copy-start(f32[1024,128]{1,0:T(8,128)} %param.7) | copy-start | bytes 1572868
  0.0 4.6 %copy-start.1 = (s32[3072]{0:T(1024)S(1)}, s32[3072]{0:T(1024)}, u32[]{:S(2)}) copy-start(s32[3072]{0:T(1024)} %param.6) | copy-start | bytes 36868
  279.2 92.1 %all-to-all-start.1 = ((bf16[1,16,240,1024]{3,1,0,2:T(8,128)(2,1)}), bf16[1,16,240,1024]{3,1,0,2:T(8,128)(2,1)}, u32[]{:S(2)}, u32[]{:S(2)}) async-start(bf16[1,16,240,1024]{3,1,0,2:T(8,128)(2,1)} %copy.17), calls=%async_computation.1 | async-start | bytes 15728640 | tf_op jit(solution)/shard_map/all_to_all | solution.py:42
where the time goes:
time: 423 us; the launch traced here: 421 us
  matrix products  115 us (27%)
  local copies, waits for them, and re-layouts  112 us (26%)
  blocking collectives  93.7 us (22%)
  waiting for transfers between devices  79.1 us (19%)
  other arithmetic  17.2 us (4%)
    all_to_all x1, blocking collectives, local_block(): recv_buf = lax.all_to_all(send_buf, 'ep', 0, 2, tiled=True)  93.7 us
    all_to_all x1, waiting for transfers between devices, local_block(): lax.all_to_all(expert_rows.reshape(1, local_experts, groups * capacity, m...  79.1 us
    dot_general x1, matrix products, local_block(): jnp.einsum('ecd,edf->ecf', rows_in, w_in, preferred_element_type=jnp.floa...  64.7 us
    dot_general x1, matrix products, local_block(): jnp.einsum('ecf,efd->ecd', hidden_act, w_out, preferred_element_type=jnp....  42 us
    gather x2, local copies, waits for them, and re-layouts, dispatch(): buffer = jnp.take(tok_rows, holder[:-1], axis=0, mode='fill', fill_value=0)  32.4 us
    gather x1, local copies, waits for them, and re-layouts, combine(): picked = jnp.take(flat_out, slot_index, axis=0, mode='fill', fill_value=0)  20.1 us
    scatter x1, local copies, waits for them, and re-layouts, dispatch(): jnp.full((num_experts * capacity + 1,), tok_count, jnp.int32).at[slot_index]  11.8 us
    all_to_all x1, local copies, waits for them, and re-layouts, local_block(): lax.all_to_all(expert_rows.reshape(1, local_experts, groups * capacity, m...  11.6 us
  transfers between devices with their start and end apart: 1, of which 1 were waited for; matrix products, arithmetic and copies ran while one was open for 2% of the time, Pallas kernels for 0%

commit v1 on v0

v1 whole, which is shorter than its diff:
```python
import functools

import jax
import jax.numpy as jnp
from jax import lax
from jax.experimental import pallas as pl
from jax.experimental.pallas import tpu as pltpu
from jax.sharding import PartitionSpec as P

MESH = pl.DeviceIdType.MESH
BF16 = jnp.bfloat16
F32 = jnp.float32

TOK = 3072
DIM = 1024
HID = 2816
NEXP = 128
NDEV = 8
LOC = NEXP // NDEV
CAP = 30
ROWS = LOC * CAP
BLK = 256
NBLK = TOK // BLK

HALF = 8 * CAP
D0 = (0, 128)
DN = (128, 112)
R0 = (0, 112)
RN = (112, 128)


def _dot(a, b, **kw):
    return jnp.dot(a, b, preferred_element_type=F32, **kw)


def _kernel(idx_ref, wr_ref, tok_hbm, win_hbm, wout_hbm, y_hbm,
            tok, key, send, recv, ret, win, wout, lhs, hid, meta, stage,
            tok_sem, win_sem, wout_sem, out_sem,
            ds_sem, dr_sem, rs_sem, rr_sem):
    me = lax.axis_index("ep")
    my_c = me % 2
    my_x = (me // 2) % 2
    my_y = me // 4

    def peer(k):
        kc = k % 2
        kx = (k // 2) % 2
        ky = k // 4
        return ((my_y + ky) % 2) * 4 + ((my_x + kx) % 2) * 2 + (my_c + kc) % 2

    tok_copy = pltpu.make_async_copy(tok_hbm, tok, tok_sem)
    tok_copy.start()

    barrier = pltpu.get_barrier_semaphore()
    for k in range(1, NDEV):
        pl.semaphore_signal(barrier, inc=1, device_id={"ep": peer(k)}, device_id_type=MESH)

    def win_copy(e):
        return pltpu.make_async_copy(win_hbm.at[e], win.at[e % 2], win_sem.at[e % 2])

    def wout_copy(e):
        return pltpu.make_async_copy(wout_hbm.at[e], wout.at[e % 2], wout_sem.at[e % 2])

    before = (lax.broadcasted_iota(jnp.int32, (BLK, BLK), 0)
              < lax.broadcasted_iota(jnp.int32, (BLK, BLK), 1)).astype(F32).astype(BF16)
    expert_col = lax.broadcasted_iota(jnp.int32, (NEXP, BLK), 0)
    carry = jnp.zeros((NEXP, 1), F32)
    for b in range(NBLK):
        idx = idx_ref[:, b * BLK:(b + 1) * BLK]
        chosen = jnp.where(expert_col == idx, 1.0, 0.0).astype(F32)
        count = _dot(chosen.astype(BF16), before) + carry
        pos = jnp.sum(chosen * count, axis=0, keepdims=True)
        carry = carry + jnp.sum(chosen, axis=1, keepdims=True)
        slot = idx.astype(F32) * CAP + pos
        key[:, b * BLK:(b + 1) * BLK] = jnp.where(pos < CAP, slot, float(NEXP * CAP))

    tok_copy.wait()
    for e in range(2):
        win_copy(e).start()
        wout_copy(e).start()
    pl.semaphore_wait(barrier, NDEV - 1)

    def d_copy(k, h, j):
        rows = pl.ds(pl.multiple_of(h * HALF + D0[j], 16), DN[j])
        return pltpu.make_async_remote_copy(
            src_ref=send.at[k - 1, rows], dst_ref=recv.at[k, rows],
            send_sem=ds_sem.at[k - 1, h * 2 + j], recv_sem=dr_sem.at[k - 1, h * 2 + j],
            device_id={"ep": peer(k)}, device_id_type=MESH)

    def r_copy(k, h, j):
        rows = pl.ds(pl.multiple_of(h * HALF + R0[j], 16), RN[j])
        return pltpu.make_async_remote_copy(
            src_ref=recv.at[k, rows], dst_ref=ret.at[k - 1, rows],
            send_sem=rs_sem.at[k - 1, h * 2 + j], recv_sem=rr_sem.at[k - 1, h * 2 + j],
            device_id={"ep": peer(k)}, device_id_type=MESH)

    row_id = lax.broadcasted_iota(jnp.int32, (BLK, 1), 0)

    def dispatch(i, _):
        q = i // 4
        p = i % 4
        h = q // 2
        j = q % 2
        first = jnp.where(p == 0, 2, jnp.where(p == 1, 3, jnp.where(p == 2, 6, 0)))
        second = jnp.where(p == 0, 4, jnp.where(p == 1, 5, jnp.where(p == 2, 7, 1)))
        start = pl.multiple_of(h * HALF + j * 128, 16)
        base_a = peer(first) * ROWS + start
        base_b = peer(second) * ROWS + start - 128
        target = (row_id + jnp.where(row_id < 128, base_a, base_b)).astype(F32)
        hid[...] = jnp.where(key[...] == target, 1.0, 0.0).astype(BF16)
        rows = pl.ds(start, 128)
        for n in range(2):
            cols = slice(n * 512, (n + 1) * 512)
            part = _dot(hid[...], tok[:, cols]).astype(BF16)

            @pl.when(p < 3)
            def _():
                send[first - 1, rows, cols] = part[:128]

            @pl.when(p == 3)
            def _():
                recv[0, rows, cols] = part[:128]

            send[second - 1, rows, cols] = part[128:]
        for jj in range(2):
            @pl.when(j == jj)
            def _():
                @pl.when(p < 3)
                def _():
                    d_copy(first, h, jj).start()
                d_copy(second, h, jj).start()
        return 0

    lax.fori_loop(0, 16, dispatch, 0)

    eye = lax.broadcasted_iota(jnp.int32, (BLK, BLK), 0) == lax.broadcasted_iota(jnp.int32, (BLK, BLK), 1)
    lane = lax.broadcasted_iota(jnp.int32, (BLK, NEXP), 1).astype(F32)

    def router(b, _):
        at = pl.ds(pl.multiple_of(b * BLK, BLK), BLK)
        logits = _dot(tok[at, :].astype(F32), wr_ref[...], precision=lax.Precision.HIGHEST)
        top = jnp.max(logits, axis=1, keepdims=True)
        weight = jnp.exp(logits - top)
        total = jnp.sum(weight, axis=1, keepdims=True)
        idx_col = jnp.sum(jnp.where(eye, idx_ref[:, at].astype(F32), 0.0), axis=1, keepdims=True)
        slot_col = jnp.sum(jnp.where(eye, key[:, at], 0.0), axis=1, keepdims=True)
        gate = jnp.sum(jnp.where(lane == idx_col, weight / total, 0.0), axis=1, keepdims=True)
        meta[at, 0:1] = slot_col
        meta[at, 1:2] = gate
        return 0

    lax.fori_loop(0, NBLK, router, 0)

    lhs[...] = jnp.zeros_like(lhs)
    order = (2, 4, 3, 5, 6, 7, 1)

    def group(g, _):
        h = g // 2
        j = g % 2
        for jj in range(2):
            @pl.when(j == jj)
            def _():
                for k in order:
                    d_copy(k, h, jj).wait_recv()

                def spread(k, _):
                    at = pl.ds(pl.multiple_of(k * 32, 32), CAP)
                    block = recv.at[k, pl.ds(pl.multiple_of(h * HALF, 16), HALF)]
                    for c in range(4):
                        lo = (jj * 4 + c) * CAP
                        lhs[c, at, :] = block[lo:lo + CAP, :]
                    return 0

                lax.fori_loop(0, NDEV, spread, 0)

        def expert(c, _):
            e = g * 4 + c
            s = e % 2
            win_copy(e).wait()
            for lo, width in ((0, 768), (768, 768), (1536, 768), (2304, 512)):
                up = _dot(lhs[c], win[s, :, lo:lo + width])
                hid[:, lo:lo + width] = jnp.maximum(up, 0.0).astype(BF16)
            wout_copy(e).wait()
            for n in range(2):
                cols = slice(n * 512, (n + 1) * 512)
                lhs[c, :, cols] = _dot(hid[:, :HID], wout[s, :, cols]).astype(BF16)

            @pl.when(e + 2 < LOC)
            def _():
                win_copy(e + 2).start()
                wout_copy(e + 2).start()
            return 0

        lax.fori_loop(0, 4, expert, 0)

        for jj in range(2):
            @pl.when(j == jj)
            def _():
                def gather(k, _):
                    at = pl.ds(pl.multiple_of(k * 32, 32), CAP)
                    block = recv.at[k, pl.ds(pl.multiple_of(h * HALF, 16), HALF)]
                    for c in range(4):
                        lo = (jj * 4 + c) * CAP
                        block[lo:lo + CAP, :] = lhs[c, at, :]
                    return 0

                lax.fori_loop(0, NDEV, gather, 0)
                for k in order:
                    r_copy(k, h, jj).start()
        return 0

    lax.fori_loop(0, 4, group, 0)

    def combine(peers, lo, n, mode):
        def block(b, _):
            at = pl.ds(pl.multiple_of(b * BLK, BLK), BLK)
            slot = meta[at, 0:1]
            total = None
            for k in peers:
                base = peer(k) * ROWS + lo
                target = (lax.broadcasted_iota(jnp.int32, (1, n), 1) + base).astype(F32)
                pick = jnp.where(slot == target, 1.0, 0.0).astype(BF16)
                rows = recv[0, lo:lo + n, :] if k == 0 else ret[k - 1, lo:lo + n, :]
                part = _dot(pick, rows)
                total = part if total is None else total + part
            if mode != "first":
                total = total + tok[at, :].astype(F32)
            if mode != "last":
                tok[at, :] = total.astype(BF16)
            else:
                s = b % 2

                @pl.when(b >= 2)
                def _():
                    pltpu.make_async_copy(stage.at[s], y_hbm.at[at], out_sem.at[s]).wait()
                stage[s] = (meta[at, 1:2] * total).astype(BF16)
                pltpu.make_async_copy(stage.at[s], y_hbm.at[at], out_sem.at[s]).start()
            return 0

        lax.fori_loop(0, NBLK, block, 0)

    for j in range(2):
        for k in order:
            r_copy(k, 0, j).wait_recv()
    combine((0, 1, 2, 3, 4, 5, 6, 7), 0, HALF, "first")
    for k in order:
        r_copy(k, 1, 0).wait_recv()
    combine((0, 1, 2, 3, 4, 5, 6, 7), HALF, RN[0], "add")
    for k in (1, 2, 4):
        r_copy(k, 1, 1).wait_recv()
    combine((0, 1, 2, 4), HALF + R0[1], RN[1], "add")
    for k in (3, 5):
        r_copy(k, 1, 1).wait_recv()
    combine((3, 5), HALF + R0[1], RN[1], "add")
    for k in (6, 7):
        r_copy(k, 1, 1).wait_recv()
    combine((6, 7), HALF + R0[1], RN[1], "last")

    for h in range(2):
        for j in range(2):
            for k in range(1, NDEV):
                d_copy(k, h, j).wait_send()
                r_copy(k, h, j).wait_send()
    for b in range(NBLK - 2, NBLK):
        at = pl.ds(b * BLK, BLK)
        pltpu.make_async_copy(stage.at[b % 2], y_hbm.at[at], out_sem.at[b % 2]).wait()


def solution(mesh):
    def local_block(tokens, expert_idx, w_router, w_in, w_out):
        any_space = pl.BlockSpec(memory_space=pl.ANY)
        vmem = pl.BlockSpec(memory_space=pltpu.VMEM)
        dma = pltpu.SemaphoreType.DMA
        return pl.pallas_call(
            _kernel,
            out_shape=jax.ShapeDtypeStruct((TOK, DIM), BF16),
            in_specs=[vmem, vmem, any_space, any_space, any_space],
            out_specs=any_space,
            scratch_shapes=[
                pltpu.VMEM((TOK, DIM), BF16),
                pltpu.VMEM((1, TOK), F32),
                pltpu.VMEM((NDEV - 1, ROWS + 16, DIM), BF16),
                pltpu.VMEM((NDEV, ROWS + 16, DIM), BF16),
                pltpu.VMEM((NDEV - 1, ROWS, DIM), BF16),
                pltpu.VMEM((2, DIM, HID), BF16),
                pltpu.VMEM((2, HID, DIM), BF16),
                pltpu.VMEM((4, BLK, DIM), BF16),
                pltpu.VMEM((BLK, TOK), BF16),
                pltpu.VMEM((TOK, 128), F32),
                pltpu.VMEM((2, BLK, DIM), BF16),
                dma, dma((2,)), dma((2,)), dma((2,)),
                dma((NDEV - 1, 4)), dma((NDEV - 1, 4)), dma((NDEV - 1, 4)), dma((NDEV - 1, 4)),
            ],
            compiler_params=pltpu.CompilerParams(
                collective_id=0, has_side_effects=True, vmem_limit_bytes=67043328),
            name="moe_step",
        )(expert_idx.reshape(1, TOK), w_router, tokens, w_in, w_out)

    return jax.shard_map(
        local_block, mesh=mesh,
        in_specs=(P(("dp", "ep"), None), P(("dp", "ep")), P(None, None), P("ep", None, None), P("ep", None, None)),
        out_specs=P(("dp", "ep"), None), check_vma=False)
```

time: 423 us -> 203 us (0.48)
  Pallas kernels: 0 us -> 196 us
  matrix products: 115 us -> 0 us
  local copies, waits for them, and re-layouts: 112 us -> 6.2 us
  blocking collectives: 93.7 us -> 0 us
  waiting for transfers between devices: 79.1 us -> 0 us
  other arithmetic: 17.2 us -> 0 us
    pallas_call x0 -> x1, Pallas kernels: none -> 196 us  [local_block(): pl.pallas_call(_kernel, out_shape=jax.ShapeDtypeStruct((TOK, DIM), BF16),...]
    dot_general x3 -> x0, matrix products: 115 us -> none  [the longest x1 64.7 us: local_block(): jnp.einsum('ecd,edf->ecf', rows_in, w_in, preferred_element_type=jnp.floa...]
    all_to_all x1 -> x0, blocking collectives: 93.7 us -> none  [local_block(): recv_buf = lax.all_to_all(send_buf, 'ep', 0, 2, tiled=True)]
    all_to_all x1 -> x0, waiting for transfers between devices: 79.1 us -> none  [local_block(): lax.all_to_all(expert_rows.reshape(1, local_experts, groups * capacity, m...]
    gather x3 -> x0, local copies, waits for them, and re-layouts: 52.5 us -> none  [the longest x2 32.4 us: dispatch(): buffer = jnp.take(tok_rows, holder[:-1], axis=0, mode='fill', fill_value=0)]
    reshape x2 -> x0, local copies, waits for them, and re-layouts: 21.9 us -> none  [the longest x1 11.2 us: local_block(): flat_out = back_buf.reshape(num_experts * capacity, model_dim)]
    scatter x1 -> x0, local copies, waits for them, and re-layouts: 11.8 us -> none  [dispatch(): jnp.full((num_experts * capacity + 1,), tok_count, jnp.int32).at[slot_index]]
    all_to_all x1 -> x0, local copies, waits for them, and re-layouts: 11.6 us -> none  [local_block(): lax.all_to_all(expert_rows.reshape(1, local_experts, groups * capacity, m...]
  transfers between devices with their start and end apart: 1 -> 0, of which waited for: 1 -> 0; matrix products, arithmetic and copies ran while one was open for 2% -> 0% of each run, Pallas kernels for 0% -> 0%
where the time goes in v1:
time: 203 us; the launch traced here: 202 us
  Pallas kernels  196 us (97%)
  local copies, waits for them, and re-layouts  6.2 us (3%)
    pallas_call x1, Pallas kernels, local_block(): pl.pallas_call(_kernel, out_shape=jax.ShapeDtypeStruct((TOK, DIM), BF16),...  196 us
    unnamed x1, local copies, waits for them, and re-layouts  6.2 us

profile of v1, /device:TPU:0, one launch (start us, length us, event | category | flops | bytes accessed | tf_op | source)
XLA Modules:
  0.0 202.0 jit_solution(9275059672953916004)
XLA Ops:
  0.0 195.8 %moe_step.1 = bf16[3072,1024]{1,0:T(8,128)(2,1)} custom-call(s32[1,3072]{1,0:T(1,128)} %bitcast.1, f32[1024,128]{1,0:T(8,128)} %wr_ref.1, bf16[3072,1024]{1,0:T(8,128)(2,1)} %tok_hbm.1, bf16[16,1024,2816]{2,1,0:T(8,128)(2,1)} %win_hbm.1, bf16[16,2816,1024]{2,1,0:T(8,128)(2,1)} %wout_hbm.1), custom_call_target="tpu_custom_call" | custom-call | tf_op jit(solution)/shard_map/moe_step/pallas_call | solution.py:274
  195.8 6.2 %copy.7 = bf16[3072,1024]{1,0:T(8,128)(2,1)} copy(bf16[3072,1024]{1,0:T(8,128)(2,1)} %moe_step.1) | data formatting | bytes 12582912

commit v2 on v1

--- a/solution.py
+++ b/solution.py
@@ -33,9 +33,9 @@
     return jnp.dot(a, b, preferred_element_type=F32, **kw)
 
 
-def _kernel(idx_ref, wr_ref, tok_hbm, win_hbm, wout_hbm, y_hbm,
-            tok, key, send, recv, ret, win, wout, lhs, hid, meta, stage,
-            tok_sem, win_sem, wout_sem, out_sem,
+def _kernel(idx_ref, wr_hbm, tok_hbm, win_hbm, wout_hbm, y_hbm,
+            tok, key, send, recv, ret, win, wout, lhs, hid, meta, stage, wr_ref,
+            wr_sem, tok_sem, win_sem, wout_sem, out_sem,
             ds_sem, dr_sem, rs_sem, rr_sem):
     me = lax.axis_index("ep")
     my_c = me % 2
@@ -75,6 +75,8 @@
         key[:, b * BLK:(b + 1) * BLK] = jnp.where(pos < CAP, slot, float(NEXP * CAP))
 
     tok_copy.wait()
+    wr_copy = pltpu.make_async_copy(wr_hbm, wr_ref, wr_sem)
+    wr_copy.start()
     for e in range(2):
         win_copy(e).start()
         wout_copy(e).start()
@@ -97,8 +99,8 @@
     row_id = lax.broadcasted_iota(jnp.int32, (BLK, 1), 0)
 
     def dispatch(i, _):
-        q = i // 4
-        p = i % 4
+        p = jnp.where(i < 8, i % 2, i // 4)
+        q = jnp.where(i < 8, i // 2, i % 4)
         h = q // 2
         j = q % 2
         first = jnp.where(p == 0, 2, jnp.where(p == 1, 3, jnp.where(p == 2, 6, 0)))
@@ -149,6 +151,7 @@
         meta[at, 1:2] = gate
         return 0
 
+    wr_copy.wait()
     lax.fori_loop(0, NBLK, router, 0)
 
     lhs[...] = jnp.zeros_like(lhs)
@@ -205,11 +208,15 @@
                     return 0
 
                 lax.fori_loop(0, NDEV, gather, 0)
-                for k in order:
+                for k in (6, 7, 1):
                     r_copy(k, h, jj).start()
         return 0
 
     lax.fori_loop(0, 4, group, 0)
+    for h in range(2):
+        for j in range(2):
+            for k in (2, 3):
+                r_copy(k, h, j).start()
 
     def combine(peers, lo, n, mode):
         def block(b, _):
@@ -239,22 +246,29 @@
 
         lax.fori_loop(0, NBLK, block, 0)
 
-    for j in range(2):
-        for k in order:
-            r_copy(k, 0, j).wait_recv()
-    combine((0, 1, 2, 3, 4, 5, 6, 7), 0, HALF, "first")
-    for k in order:
-        r_copy(k, 1, 0).wait_recv()
-    combine((0, 1, 2, 3, 4, 5, 6, 7), HALF, RN[0], "add")
-    for k in (1, 2, 4):
-        r_copy(k, 1, 1).wait_recv()
-    combine((0, 1, 2, 4), HALF + R0[1], RN[1], "add")
-    for k in (3, 5):
-        r_copy(k, 1, 1).wait_recv()
-    combine((3, 5), HALF + R0[1], RN[1], "add")
-    for k in (6, 7):
-        r_copy(k, 1, 1).wait_recv()
-    combine((6, 7), HALF + R0[1], RN[1], "last")
+    def arrived(peers, *chunks):
+        for h, j in chunks:
+            for k in peers:
+                r_copy(k, h, j).wait_recv()
+
+    arrived((1,), (0, 0), (0, 1), (1, 0), (1, 1))
+    combine((0, 1), 0, ROWS, "first")
+    arrived((6, 7), (0, 0), (0, 1))
+    combine((6, 7), 0, HALF, "add")
+    arrived((6, 7), (1, 0), (1, 1))
+    for h in range(2):
+        for j in range(2):
+            for k in (4, 5):
+                r_copy(k, h, j).start()
+    combine((6, 7), HALF, HALF, "add")
+    arrived((2, 3, 4, 5), (0, 0), (0, 1))
+    combine((2, 3, 4, 5), 0, HALF, "add")
+    arrived((2, 3, 4, 5), (1, 0))
+    combine((2, 3, 4, 5), HALF, RN[0], "add")
+    arrived((2, 4), (1, 1))
+    combine((2, 4), HALF + R0[1], RN[1], "add")
+    arrived((3, 5), (1, 1))
+    combine((3, 5), HALF + R0[1], RN[1], "last")
 
     for h in range(2):
         for j in range(2):
@@ -274,7 +288,7 @@
         return pl.pallas_call(
             _kernel,
             out_shape=jax.ShapeDtypeStruct((TOK, DIM), BF16),
-            in_specs=[vmem, vmem, any_space, any_space, any_space],
+            in_specs=[vmem, any_space, any_space, any_space, any_space],
             out_specs=any_space,
             scratch_shapes=[
                 pltpu.VMEM((TOK, DIM), BF16),
@@ -288,7 +302,8 @@
                 pltpu.VMEM((BLK, TOK), BF16),
                 pltpu.VMEM((TOK, 128), F32),
                 pltpu.VMEM((2, BLK, DIM), BF16),
-                dma, dma((2,)), dma((2,)), dma((2,)),
+                pltpu.VMEM((DIM, NEXP), F32),
+                dma, dma, dma((2,)), dma((2,)), dma((2,)),
                 dma((NDEV - 1, 4)), dma((NDEV - 1, 4)), dma((NDEV - 1, 4)), dma((NDEV - 1, 4)),
             ],
             compiler_params=pltpu.CompilerParams(

time: 203 us -> 200 us (0.985)
  no operation moved by 1% of the time
where the time goes in v2:
time: 200 us
  Pallas kernels  194 us (97%)
  local copies, waits for them, and re-layouts  6.2 us (3%)
    pallas_call x1, Pallas kernels, local_block(): pl.pallas_call(_kernel, out_shape=jax.ShapeDtypeStruct((TOK, DIM), BF16),...  194 us
    unnamed x1, local copies, waits for them, and re-layouts  6.2 us

profile of v2, /device:TPU:0, one launch (start us, length us, event | category | flops | bytes accessed | tf_op | source)
XLA Modules:
  0.0 200.1 jit_solution(15679308737517404809)
XLA Ops:
  0.0 193.9 %moe_step.1 = bf16[3072,1024]{1,0:T(8,128)(2,1)} custom-call(s32[1,3072]{1,0:T(1,128)} %bitcast.1, f32[1024,128]{1,0:T(8,128)} %wr_hbm.1, bf16[3072,1024]{1,0:T(8,128)(2,1)} %tok_hbm.1, bf16[16,1024,2816]{2,1,0:T(8,128)(2,1)} %win_hbm.1, bf16[16,2816,1024]{2,1,0:T(8,128)(2,1)} %wout_hbm.1), custom_call_target="tpu_custom_call" | custom-call | tf_op jit(solution)/shard_map/moe_step/pallas_call | solution.py:288
  193.9 6.2 %copy.7 = bf16[3072,1024]{1,0:T(8,128)(2,1)} copy(bf16[3072,1024]{1,0:T(8,128)(2,1)} %moe_step.1) | data formatting | bytes 12582912

commit v3 on v2

--- a/solution.py
+++ b/solution.py
@@ -27,26 +27,35 @@
 DN = (128, 112)
 R0 = (0, 112)
 RN = (112, 128)
+LAST = HALF + R0[1]
 
 
 def _dot(a, b, **kw):
     return jnp.dot(a, b, preferred_element_type=F32, **kw)
 
 
-def _kernel(idx_ref, wr_hbm, tok_hbm, win_hbm, wout_hbm, y_hbm,
-            tok, key, send, recv, ret, win, wout, lhs, hid, meta, stage, wr_ref,
-            wr_sem, tok_sem, win_sem, wout_sem, out_sem,
+def _peer(me, k):
+    return (((me // 4 + k // 4) % 2) * 4
+            + (((me // 2) % 2 + (k // 2) % 2) % 2) * 2 + (me % 2 + k % 2) % 2)
+
+
+def _pick(slot, pieces):
+    total = None
+    for base, rows in pieces:
+        target = (lax.broadcasted_iota(jnp.int32, (1, rows.shape[0]), 1) + base).astype(F32)
+        part = _dot(jnp.where(slot == target, 1.0, 0.0).astype(BF16), rows[...])
+        total = part if total is None else total + part
+    return total
+
+
+def _kernel(idx_ref, wr_hbm, tok_hbm, win_hbm, wout_hbm, y_hbm, meta_hbm, last_hbm,
+            tok, key, send, recv, ret, win, wout, lhs, hid, meta, wr_ref,
+            wr_sem, tok_sem, y_sem, meta_sem, last_sem, win_sem, wout_sem,
             ds_sem, dr_sem, rs_sem, rr_sem):
     me = lax.axis_index("ep")
-    my_c = me % 2
-    my_x = (me // 2) % 2
-    my_y = me // 4
 
     def peer(k):
-        kc = k % 2
-        kx = (k // 2) % 2
-        ky = k // 4
-        return ((my_y + ky) % 2) * 4 + ((my_x + kx) % 2) * 2 + (my_c + kc) % 2
+        return _peer(me, k)
 
     tok_copy = pltpu.make_async_copy(tok_hbm, tok, tok_sem)
     tok_copy.start()
@@ -96,11 +105,14 @@
             send_sem=rs_sem.at[k - 1, h * 2 + j], recv_sem=rr_sem.at[k - 1, h * 2 + j],
             device_id={"ep": peer(k)}, device_id_type=MESH)
 
+    order = (6, 7, 2, 4, 3, 5, 1)
+    far = order[:-1]
+
     row_id = lax.broadcasted_iota(jnp.int32, (BLK, 1), 0)
 
     def dispatch(i, _):
-        p = jnp.where(i < 8, i % 2, i // 4)
-        q = jnp.where(i < 8, i // 2, i % 4)
+        q = i // 4
+        p = i % 4
         h = q // 2
         j = q % 2
         first = jnp.where(p == 0, 2, jnp.where(p == 1, 3, jnp.where(p == 2, 6, 0)))
@@ -125,12 +137,12 @@
 
             send[second - 1, rows, cols] = part[128:]
         for jj in range(2):
-            @pl.when(j == jj)
+            @pl.when(i // 4 == jj)
             def _():
                 @pl.when(p < 3)
                 def _():
-                    d_copy(first, h, jj).start()
-                d_copy(second, h, jj).start()
+                    d_copy(first, 0, jj).start()
+                d_copy(second, 0, jj).start()
         return 0
 
     lax.fori_loop(0, 16, dispatch, 0)
@@ -152,10 +164,14 @@
         return 0
 
     wr_copy.wait()
-    lax.fori_loop(0, NBLK, router, 0)
+    lax.fori_loop(0, NBLK // 2, router, 0)
+    for k in order:
+        d_copy(k, 1, 0).start()
+    lax.fori_loop(NBLK // 2, NBLK, router, 0)
+    for k in order:
+        d_copy(k, 1, 1).start()
 
     lhs[...] = jnp.zeros_like(lhs)
-    order = (2, 4, 3, 5, 6, 7, 1)
 
     def group(g, _):
         h = g // 2
@@ -165,6 +181,12 @@
             def _():
                 for k in order:
                     d_copy(k, h, jj).wait_recv()
+
+                @pl.when(h == 1)
+                def _():
+                    if jj == 0:
+                        for k in far:
+                            r_copy(k, 0, 1).start()
 
                 def spread(k, _):
                     at = pl.ds(pl.multiple_of(k * 32, 32), CAP)
@@ -208,40 +230,35 @@
                     return 0
 
                 lax.fori_loop(0, NDEV, gather, 0)
-                for k in (6, 7, 1):
-                    r_copy(k, h, jj).start()
+                r_copy(1, h, jj).start()
+                if jj == 1:
+                    @pl.when(h == 0)
+                    def _():
+                        for k in far:
+                            r_copy(k, 0, 0).start()
         return 0
 
     lax.fori_loop(0, 4, group, 0)
-    for h in range(2):
-        for j in range(2):
-            for k in (2, 3):
-                r_copy(k, h, j).start()
-
-    def combine(peers, lo, n, mode):
+    for k in far:
+        r_copy(k, 1, 0).start()
+
+    def y_copy(b):
+        at = pl.ds(pl.multiple_of(b * BLK, BLK), BLK)
+        return pltpu.make_async_copy(tok.at[at], y_hbm.at[at], y_sem.at[b])
+
+    def combine(pieces, first=False, last=False):
         def block(b, _):
+            if last:
+                @pl.when(b >= 1)
+                def _():
+                    y_copy(b - 1).start()
             at = pl.ds(pl.multiple_of(b * BLK, BLK), BLK)
-            slot = meta[at, 0:1]
-            total = None
-            for k in peers:
-                base = peer(k) * ROWS + lo
-                target = (lax.broadcasted_iota(jnp.int32, (1, n), 1) + base).astype(F32)
-                pick = jnp.where(slot == target, 1.0, 0.0).astype(BF16)
-                rows = recv[0, lo:lo + n, :] if k == 0 else ret[k - 1, lo:lo + n, :]
-                part = _dot(pick, rows)
-                total = part if total is None else total + part
-            if mode != "first":
+            total = _pick(meta[at, 0:1], [
+                (peer(k) * ROWS + lo, recv.at[0, lo:lo + n] if k == 0 else ret.at[k - 1, lo:lo + n])
+                for k, lo, n in pieces])
+            if not first:
                 total = total + tok[at, :].astype(F32)
-            if mode != "last":
-                tok[at, :] = total.astype(BF16)
-            else:
-                s = b % 2
-
-                @pl.when(b >= 2)
-                def _():
-                    pltpu.make_async_copy(stage.at[s], y_hbm.at[at], out_sem.at[s]).wait()
-                stage[s] = (meta[at, 1:2] * total).astype(BF16)
-                pltpu.make_async_copy(stage.at[s], y_hbm.at[at], out_sem.at[s]).start()
+            tok[at, :] = total.astype(BF16)
             return 0
 
         lax.fori_loop(0, NBLK, block, 0)
@@ -251,33 +268,39 @@
             for k in peers:
                 r_copy(k, h, j).wait_recv()
 
+    meta_copy = pltpu.make_async_copy(meta, meta_hbm, meta_sem)
+    meta_copy.start()
     arrived((1,), (0, 0), (0, 1), (1, 0), (1, 1))
-    combine((0, 1), 0, ROWS, "first")
-    arrived((6, 7), (0, 0), (0, 1))
-    combine((6, 7), 0, HALF, "add")
-    arrived((6, 7), (1, 0), (1, 1))
-    for h in range(2):
-        for j in range(2):
-            for k in (4, 5):
-                r_copy(k, h, j).start()
-    combine((6, 7), HALF, HALF, "add")
-    arrived((2, 3, 4, 5), (0, 0), (0, 1))
-    combine((2, 3, 4, 5), 0, HALF, "add")
-    arrived((2, 3, 4, 5), (1, 0))
-    combine((2, 3, 4, 5), HALF, RN[0], "add")
-    arrived((2, 4), (1, 1))
-    combine((2, 4), HALF + R0[1], RN[1], "add")
-    arrived((3, 5), (1, 1))
-    combine((3, 5), HALF + R0[1], RN[1], "last")
+    combine([(0, 0, ROWS), (1, 0, ROWS)], first=True)
+    arrived(far, (0, 0))
+    for k in far:
+        r_copy(k, 1, 1).start()
+    arrived(far, (0, 1))
+    combine([(k, 0, HALF) for k in far])
+    arrived(far, (1, 0))
+    arrived((6, 7), (1, 1))
+    combine([(k, HALF, RN[0]) for k in far] + [(k, LAST, RN[1]) for k in (6, 7)], last=True)
+    arrived((2, 3, 4, 5), (1, 1))
+    y_copy(NBLK - 1).start()
+    last_copy = pltpu.make_async_copy(ret.at[1:5, LAST:ROWS], last_hbm, last_sem)
+    last_copy.start()
 
     for h in range(2):
         for j in range(2):
             for k in range(1, NDEV):
                 d_copy(k, h, j).wait_send()
                 r_copy(k, h, j).wait_send()
-    for b in range(NBLK - 2, NBLK):
-        at = pl.ds(b * BLK, BLK)
-        pltpu.make_async_copy(stage.at[b % 2], y_hbm.at[at], out_sem.at[b % 2]).wait()
+    for b in range(NBLK):
+        y_copy(b).wait()
+    meta_copy.wait()
+    last_copy.wait()
+
+
+def _finish(y_ref, meta_ref, last_ref, out_ref):
+    me = lax.axis_index("ep")
+    total = _pick(meta_ref[:, 0:1], [(_peer(me, k) * ROWS + LAST, last_ref.at[k - 2]) for k in range(2, 6)])
+    total = total + y_ref[...].astype(F32)
+    out_ref[...] = (meta_ref[:, 1:2] * total).astype(BF16)
 
 
 def solution(mesh):
@@ -285,11 +308,13 @@
         any_space = pl.BlockSpec(memory_space=pl.ANY)
         vmem = pl.BlockSpec(memory_space=pltpu.VMEM)
         dma = pltpu.SemaphoreType.DMA
-        return pl.pallas_call(
+        partial, meta, last = pl.pallas_call(
             _kernel,
-            out_shape=jax.ShapeDtypeStruct((TOK, DIM), BF16),
+            out_shape=(jax.ShapeDtypeStruct((TOK, DIM), BF16),
+                       jax.ShapeDtypeStruct((TOK, 128), F32),
+                       jax.ShapeDtypeStruct((4, RN[1], DIM), BF16)),
             in_specs=[vmem, any_space, any_space, any_space, any_space],
-            out_specs=any_space,
+            out_specs=(any_space,) * 3,
             scratch_shapes=[
                 pltpu.VMEM((TOK, DIM), BF16),
                 pltpu.VMEM((1, TOK), F32),
@@ -301,15 +326,25 @@
                 pltpu.VMEM((4, BLK, DIM), BF16),
                 pltpu.VMEM((BLK, TOK), BF16),
                 pltpu.VMEM((TOK, 128), F32),
-                pltpu.VMEM((2, BLK, DIM), BF16),
                 pltpu.VMEM((DIM, NEXP), F32),
-                dma, dma, dma((2,)), dma((2,)), dma((2,)),
+                dma, dma, dma((NBLK,)), dma, dma, dma((2,)), dma((2,)),
                 dma((NDEV - 1, 4)), dma((NDEV - 1, 4)), dma((NDEV - 1, 4)), dma((NDEV - 1, 4)),
             ],
             compiler_params=pltpu.CompilerParams(
                 collective_id=0, has_side_effects=True, vmem_limit_bytes=67043328),
             name="moe_step",
         )(expert_idx.reshape(1, TOK), w_router, tokens, w_in, w_out)
+        return pl.pallas_call(
+            _finish,
+            grid=(NBLK,),
+            out_shape=jax.ShapeDtypeStruct((TOK, DIM), BF16),
+            in_specs=[pl.BlockSpec((BLK, DIM), lambda b: (b, 0)),
+                      pl.BlockSpec((BLK, 128), lambda b: (b, 0)),
+                      pl.BlockSpec((4, RN[1], DIM), lambda b: (0, 0, 0))],
+            out_specs=pl.BlockSpec((BLK, DIM), lambda b: (b, 0)),
+            compiler_params=pltpu.CompilerParams(dimension_semantics=("arbitrary",)),
+            name="moe_finish",
+        )(partial, meta, last)
 
     return jax.shard_map(
         local_block, mesh=mesh,

time: 200 us -> 200 us (level)
  local copies, waits for them, and re-layouts: 6.2 us -> 0 us
  Pallas kernels: 194 us -> 199 us
    unnamed x1 -> x0, local copies, waits for them, and re-layouts: 6.2 us -> none
    pallas_call x1 -> x2, Pallas kernels: 194 us -> 199 us  [the longest x1 185 us: local_block(): pl.pallas_call(_kernel, out_shape=(jax.ShapeDtypeStruct((TOK, DIM), BF16)...]
where the time goes in v3:
time: 200 us; the launch traced here: 199 us
  Pallas kernels  199 us (100%)
    pallas_call x1, Pallas kernels, local_block(): pl.pallas_call(_kernel, out_shape=(jax.ShapeDtypeStruct((TOK, DIM), BF16)...  185 us
    pallas_call x1, Pallas kernels, local_block(): pl.pallas_call(_finish, grid=(NBLK,), out_shape=jax.ShapeDtypeStruct((TOK...  14.1 us

profile of v3, /device:TPU:0, one launch (start us, length us, event | category | flops | bytes accessed | tf_op | source)
XLA Modules:
  0.0 199.2 jit_solution(1987306263241959597)
XLA Ops:
  0.0 185.1 %moe_step.1 = (bf16[3072,1024]{1,0:T(8,128)(2,1)}, f32[3072,128]{1,0:T(8,128)}, bf16[4,128,1024]{2,1,0:T(8,128)(2,1)}) custom-call(s32[1,3072]{1,0:T(1,128)} %bitcast.1, f32[1024,128]{1,0:T(8,128)} %wr_hbm.1, bf16[3072,1024]{1,0:T(8,128)(2,1)} %tok_hbm.1, bf16[16,1024,2816]{2,1,0:T(8,128)(2,1)} %win_hbm.1, bf16[16,2816,1024]{2,1,0:T(8,128)(2,1)} %wout_hbm.1), custom_call_target="tpu_custom_call" | custom-call | tf_op jit(solution)/shard_map/moe_step/pallas_call | solution.py:311
  185.1 14.1 %moe_finish.1 = bf16[3072,1024]{1,0:T(8,128)(2,1)} custom-call(bf16[3072,1024]{1,0:T(8,128)(2,1)} %get-tuple-element.8.y_ref, f32[3072,128]{1,0:T(8,128)} %get-tuple-element.9.meta_ref, bf16[4,128,1024]{2,1,0:T(8,128)(2,1)} %get-tuple-element.10.last_ref), custom_call_target="tpu_custom_call" | custom-call | tf_op jit(solution)/shard_map/moe_finish/pallas_call | solution.py:337

commit v4 on v3

--- a/solution.py
+++ b/solution.py
@@ -236,11 +236,19 @@
                     def _():
                         for k in far:
                             r_copy(k, 0, 0).start()
+
+                    @pl.when(h == 1)
+                    def _():
+                        for k in (6, 7):
+                            r_copy(k, 1, 1).start()
+                else:
+                    @pl.when(h == 1)
+                    def _():
+                        for k in far:
+                            r_copy(k, 1, 0).start()
         return 0
 
     lax.fori_loop(0, 4, group, 0)
-    for k in far:
-        r_copy(k, 1, 0).start()
 
     def y_copy(b):
         at = pl.ds(pl.multiple_of(b * BLK, BLK), BLK)
@@ -272,12 +280,11 @@
     meta_copy.start()
     arrived((1,), (0, 0), (0, 1), (1, 0), (1, 1))
     combine([(0, 0, ROWS), (1, 0, ROWS)], first=True)
-    arrived(far, (0, 0))
-    for k in far:
-        r_copy(k, 1, 1).start()
-    arrived(far, (0, 1))
+    arrived(far, (0, 0), (0, 1))
     combine([(k, 0, HALF) for k in far])
     arrived(far, (1, 0))
+    for k in (2, 4, 3, 5):
+        r_copy(k, 1, 1).start()
     arrived((6, 7), (1, 1))
     combine([(k, HALF, RN[0]) for k in far] + [(k, LAST, RN[1]) for k in (6, 7)], last=True)
     arrived((2, 3, 4, 5), (1, 1))
@@ -296,11 +303,38 @@
     last_copy.wait()
 
 
-def _finish(y_ref, meta_ref, last_ref, out_ref):
+def _finish(y_hbm, meta_hbm, last_hbm, out_hbm, y, meta, last, out, y_sem, meta_sem, last_sem, out_sem):
     me = lax.axis_index("ep")
-    total = _pick(meta_ref[:, 0:1], [(_peer(me, k) * ROWS + LAST, last_ref.at[k - 2]) for k in range(2, 6)])
-    total = total + y_ref[...].astype(F32)
-    out_ref[...] = (meta_ref[:, 1:2] * total).astype(BF16)
+
+    def rows(b):
+        return pl.ds(pl.multiple_of(b * BLK, BLK), BLK)
+
+    def y_copy(b):
+        return pltpu.make_async_copy(y_hbm.at[rows(b)], y.at[rows(b)], y_sem.at[b])
+
+    def out_copy(b):
+        return pltpu.make_async_copy(out.at[rows(b)], out_hbm.at[rows(b)], out_sem.at[b])
+
+    last_copy = pltpu.make_async_copy(last_hbm, last, last_sem)
+    meta_copy = pltpu.make_async_copy(meta_hbm, meta, meta_sem)
+    last_copy.start()
+    meta_copy.start()
+    for b in range(NBLK):
+        y_copy(b).start()
+    last_copy.wait()
+    meta_copy.wait()
+
+    def block(b, _):
+        y_copy(b).wait()
+        total = _pick(meta[rows(b), 0:1], [(_peer(me, k) * ROWS + LAST, last.at[k - 2]) for k in range(2, 6)])
+        total = total + y[rows(b), :].astype(F32)
+        out[rows(b), :] = (meta[rows(b), 1:2] * total).astype(BF16)
+        out_copy(b).start()
+        return 0
+
+    lax.fori_loop(0, NBLK, block, 0)
+    for b in range(NBLK):
+        out_copy(b).wait()
 
 
 def solution(mesh):
@@ -336,13 +370,17 @@
         )(expert_idx.reshape(1, TOK), w_router, tokens, w_in, w_out)
         return pl.pallas_call(
             _finish,
-            grid=(NBLK,),
             out_shape=jax.ShapeDtypeStruct((TOK, DIM), BF16),
-            in_specs=[pl.BlockSpec((BLK, DIM), lambda b: (b, 0)),
-                      pl.BlockSpec((BLK, 128), lambda b: (b, 0)),
-                      pl.BlockSpec((4, RN[1], DIM), lambda b: (0, 0, 0))],
-            out_specs=pl.BlockSpec((BLK, DIM), lambda b: (b, 0)),
-            compiler_params=pltpu.CompilerParams(dimension_semantics=("arbitrary",)),
+            in_specs=[any_space] * 3,
+            out_specs=any_space,
+            scratch_shapes=[
+                pltpu.VMEM((TOK, DIM), BF16),
+                pltpu.VMEM((TOK, 128), F32),
+                pltpu.VMEM((4, RN[1], DIM), BF16),
+                pltpu.VMEM((TOK, DIM), BF16),
+                dma((NBLK,)), dma, dma, dma((NBLK,)),
+            ],
+            compiler_params=pltpu.CompilerParams(vmem_limit_bytes=60 * 2**20),
             name="moe_finish",
         )(partial, meta, last)
 

time: 200 us -> 199 us (level)
  no operation moved by 1% of the time
where the time goes in v4:
time: 199 us
  Pallas kernels  199 us (100%)
    pallas_call x1, Pallas kernels, local_block(): pl.pallas_call(_kernel, out_shape=(jax.ShapeDtypeStruct((TOK, DIM), BF16)...  185 us
    pallas_call x1, Pallas kernels, local_block(): pl.pallas_call(_finish, out_shape=jax.ShapeDtypeStruct((TOK, DIM), BF16),...  13.5 us

profile of v4, /device:TPU:0, one launch (start us, length us, event | category | flops | bytes accessed | tf_op | source)
XLA Modules:
  0.0 198.6 jit_solution(9798926910740801523)
XLA Ops:
  0.0 185.1 %moe_step.1 = (bf16[3072,1024]{1,0:T(8,128)(2,1)}, f32[3072,128]{1,0:T(8,128)}, bf16[4,128,1024]{2,1,0:T(8,128)(2,1)}) custom-call(s32[1,3072]{1,0:T(1,128)} %bitcast.1, f32[1024,128]{1,0:T(8,128)} %wr_hbm.1, bf16[3072,1024]{1,0:T(8,128)(2,1)} %tok_hbm.1, bf16[16,1024,2816]{2,1,0:T(8,128)(2,1)} %win_hbm.1, bf16[16,2816,1024]{2,1,0:T(8,128)(2,1)} %wout_hbm.1), custom_call_target="tpu_custom_call" | custom-call | tf_op jit(solution)/shard_map/moe_step/pallas_call | solution.py:345
  185.1 13.5 %moe_finish.1 = bf16[3072,1024]{1,0:T(8,128)(2,1)} custom-call(bf16[3072,1024]{1,0:T(8,128)(2,1)} %get-tuple-element.8.y_hbm, f32[3072,128]{1,0:T(8,128)} %get-tuple-element.9.meta_hbm, bf16[4,128,1024]{2,1,0:T(8,128)(2,1)} %get-tuple-element.10.last_hbm), custom_call_target="tpu_custom_call" | custom-call | tf_op jit(solution)/shard_map/moe_finish/pallas_call | solution.py:371

commit v5 on v4

--- a/solution.py
+++ b/solution.py
@@ -39,17 +39,28 @@
             + (((me // 2) % 2 + (k // 2) % 2) % 2) * 2 + (me % 2 + k % 2) % 2)
 
 
-def _pick(slot, pieces):
+def _targets(me, pieces):
+    width = sum(n for _, _, n in pieces)
+    row = lax.broadcasted_iota(jnp.int32, (1, width), 1)
+    shift = None
+    start = 0
+    for k, lo, n in pieces:
+        here = _peer(me, k) * ROWS + lo - start
+        shift = jnp.full((1, width), here) if shift is None else jnp.where(row >= start, here, shift)
+        start += n
+    return (row + shift).astype(F32)
+
+
+def _pick(slot, sources):
     total = None
-    for base, rows in pieces:
-        target = (lax.broadcasted_iota(jnp.int32, (1, rows.shape[0]), 1) + base).astype(F32)
+    for target, rows in sources:
         part = _dot(jnp.where(slot == target, 1.0, 0.0).astype(BF16), rows[...])
         total = part if total is None else total + part
     return total
 
 
 def _kernel(idx_ref, wr_hbm, tok_hbm, win_hbm, wout_hbm, y_hbm, meta_hbm, last_hbm,
-            tok, key, send, recv, ret, win, wout, lhs, hid, meta, wr_ref,
+            tok, key, send, recv, ret_p, ret_a, ret_b, ret_c, win, wout, lhs, hid, meta, wr_ref, wr3,
             wr_sem, tok_sem, y_sem, meta_sem, last_sem, win_sem, wout_sem,
             ds_sem, dr_sem, rs_sem, rr_sem):
     me = lax.axis_index("ep")
@@ -98,10 +109,21 @@
             send_sem=ds_sem.at[k - 1, h * 2 + j], recv_sem=dr_sem.at[k - 1, h * 2 + j],
             device_id={"ep": peer(k)}, device_id_type=MESH)
 
+    def landing(k, h, j):
+        if k == 1:
+            return ret_p.at[pl.ds(pl.multiple_of(h * HALF + R0[j], 16), RN[j])]
+        if h == 0:
+            return ret_a.at[pl.ds((k - 2) * HALF + R0[j], RN[j])]
+        if j == 0:
+            return ret_b.at[pl.ds((k - 2) * RN[0], RN[0])]
+        if k >= 6:
+            return ret_b.at[pl.ds(6 * RN[0] + (k - 6) * RN[1], RN[1])]
+        return ret_c.at[pl.ds((k - 2) * RN[1], RN[1])]
+
     def r_copy(k, h, j):
         rows = pl.ds(pl.multiple_of(h * HALF + R0[j], 16), RN[j])
         return pltpu.make_async_remote_copy(
-            src_ref=recv.at[k, rows], dst_ref=ret.at[k - 1, rows],
+            src_ref=recv.at[k, rows], dst_ref=landing(k, h, j),
             send_sem=rs_sem.at[k - 1, h * 2 + j], recv_sem=rr_sem.at[k - 1, h * 2 + j],
             device_id={"ep": peer(k)}, device_id_type=MESH)
 
@@ -136,13 +158,17 @@
                 recv[0, rows, cols] = part[:128]
 
             send[second - 1, rows, cols] = part[128:]
-        for jj in range(2):
-            @pl.when(i // 4 == jj)
-            def _():
-                @pl.when(p < 3)
-                def _():
-                    d_copy(first, 0, jj).start()
-                d_copy(second, 0, jj).start()
+        @pl.when(i < 4)
+        def _():
+            @pl.when(p < 3)
+            def _():
+                d_copy(first, 0, 0).start()
+            d_copy(second, 0, 0).start()
+
+        @pl.when(i == 10)
+        def _():
+            for k in order:
+                d_copy(k, 0, 1).start()
         return 0
 
     lax.fori_loop(0, 16, dispatch, 0)
@@ -152,7 +178,8 @@
 
     def router(b, _):
         at = pl.ds(pl.multiple_of(b * BLK, BLK), BLK)
-        logits = _dot(tok[at, :].astype(F32), wr_ref[...], precision=lax.Precision.HIGHEST)
+        parts = _dot(tok[at, :], wr3[...])
+        logits = parts[:, :NEXP] + parts[:, NEXP:2 * NEXP] + parts[:, 2 * NEXP:]
         top = jnp.max(logits, axis=1, keepdims=True)
         weight = jnp.exp(logits - top)
         total = jnp.sum(weight, axis=1, keepdims=True)
@@ -164,29 +191,28 @@
         return 0
 
     wr_copy.wait()
-    lax.fori_loop(0, NBLK // 2, router, 0)
-    for k in order:
-        d_copy(k, 1, 0).start()
-    lax.fori_loop(NBLK // 2, NBLK, router, 0)
-    for k in order:
-        d_copy(k, 1, 1).start()
+    top_bf16 = float(jnp.finfo(BF16).max)
+    rest = wr_ref[...]
+    for n in range(3):
+        part = jnp.clip(rest, -top_bf16, top_bf16).astype(BF16)
+        wr3[:, n * NEXP:(n + 1) * NEXP] = part
+        rest = rest - part.astype(F32)
 
     lhs[...] = jnp.zeros_like(lhs)
 
     def group(g, _):
         h = g // 2
         j = g % 2
+
+        @pl.when(g == 2)
+        def _():
+            lax.fori_loop(0, NBLK, router, 0)
+
         for jj in range(2):
             @pl.when(j == jj)
             def _():
                 for k in order:
                     d_copy(k, h, jj).wait_recv()
-
-                @pl.when(h == 1)
-                def _():
-                    if jj == 0:
-                        for k in far:
-                            r_copy(k, 0, 1).start()
 
                 def spread(k, _):
                     at = pl.ds(pl.multiple_of(k * 32, 32), CAP)
@@ -214,6 +240,26 @@
             def _():
                 win_copy(e + 2).start()
                 wout_copy(e + 2).start()
+
+            @pl.when(e == 1)
+            def _():
+                for k in order:
+                    d_copy(k, 1, 0).start()
+
+            @pl.when(e == 7)
+            def _():
+                for k in order:
+                    d_copy(k, 1, 1).start()
+
+            @pl.when(e == 10)
+            def _():
+                for k in far:
+                    r_copy(k, 0, 0).start()
+
+            @pl.when(e == 14)
+            def _():
+                for k in far:
+                    r_copy(k, 0, 1).start()
             return 0
 
         lax.fori_loop(0, 4, expert, 0)
@@ -231,21 +277,6 @@
 
                 lax.fori_loop(0, NDEV, gather, 0)
                 r_copy(1, h, jj).start()
-                if jj == 1:
-                    @pl.when(h == 0)
-                    def _():
-                        for k in far:
-                            r_copy(k, 0, 0).start()
-
-                    @pl.when(h == 1)
-                    def _():
-                        for k in (6, 7):
-                            r_copy(k, 1, 1).start()
-                else:
-                    @pl.when(h == 1)
-                    def _():
-                        for k in far:
-                            r_copy(k, 1, 0).start()
         return 0
 
     lax.fori_loop(0, 4, group, 0)
@@ -254,16 +285,16 @@
         at = pl.ds(pl.multiple_of(b * BLK, BLK), BLK)
         return pltpu.make_async_copy(tok.at[at], y_hbm.at[at], y_sem.at[b])
 
-    def combine(pieces, first=False, last=False):
+    def combine(sources, first=False, last=False):
+        sources = [(_targets(me, pieces), rows) for pieces, rows in sources]
+
         def block(b, _):
             if last:
                 @pl.when(b >= 1)
                 def _():
                     y_copy(b - 1).start()
             at = pl.ds(pl.multiple_of(b * BLK, BLK), BLK)
-            total = _pick(meta[at, 0:1], [
-                (peer(k) * ROWS + lo, recv.at[0, lo:lo + n] if k == 0 else ret.at[k - 1, lo:lo + n])
-                for k, lo, n in pieces])
+            total = _pick(meta[at, 0:1], sources)
             if not first:
                 total = total + tok[at, :].astype(F32)
             tok[at, :] = total.astype(BF16)
@@ -279,17 +310,22 @@
     meta_copy = pltpu.make_async_copy(meta, meta_hbm, meta_sem)
     meta_copy.start()
     arrived((1,), (0, 0), (0, 1), (1, 0), (1, 1))
-    combine([(0, 0, ROWS), (1, 0, ROWS)], first=True)
-    arrived(far, (0, 0), (0, 1))
-    combine([(k, 0, HALF) for k in far])
-    arrived(far, (1, 0))
+    combine([([(0, 0, ROWS)], recv.at[0, :ROWS]), ([(1, 0, ROWS)], ret_p)], first=True)
+    arrived(far, (0, 0))
+    for k in far:
+        r_copy(k, 1, 0).start()
+    arrived(far, (0, 1))
+    for k in (6, 7):
+        r_copy(k, 1, 1).start()
+    combine([([(k, 0, HALF) for k in range(2, 8)], ret_a)])
     for k in (2, 4, 3, 5):
         r_copy(k, 1, 1).start()
+    arrived(far, (1, 0))
     arrived((6, 7), (1, 1))
-    combine([(k, HALF, RN[0]) for k in far] + [(k, LAST, RN[1]) for k in (6, 7)], last=True)
+    combine([([(k, HALF, RN[0]) for k in range(2, 8)] + [(k, LAST, RN[1]) for k in (6, 7)], ret_b)], last=True)
     arrived((2, 3, 4, 5), (1, 1))
     y_copy(NBLK - 1).start()
-    last_copy = pltpu.make_async_copy(ret.at[1:5, LAST:ROWS], last_hbm, last_sem)
+    last_copy = pltpu.make_async_copy(ret_c, last_hbm, last_sem)
     last_copy.start()
 
     for h in range(2):
@@ -321,12 +357,13 @@
     meta_copy.start()
     for b in range(NBLK):
         y_copy(b).start()
+    target = _targets(me, [(k, LAST, RN[1]) for k in range(2, 6)])
     last_copy.wait()
     meta_copy.wait()
 
     def block(b, _):
         y_copy(b).wait()
-        total = _pick(meta[rows(b), 0:1], [(_peer(me, k) * ROWS + LAST, last.at[k - 2]) for k in range(2, 6)])
+        total = _pick(meta[rows(b), 0:1], [(target, last)])
         total = total + y[rows(b), :].astype(F32)
         out[rows(b), :] = (meta[rows(b), 1:2] * total).astype(BF16)
         out_copy(b).start()
@@ -346,7 +383,7 @@
             _kernel,
             out_shape=(jax.ShapeDtypeStruct((TOK, DIM), BF16),
                        jax.ShapeDtypeStruct((TOK, 128), F32),
-                       jax.ShapeDtypeStruct((4, RN[1], DIM), BF16)),
+                       jax.ShapeDtypeStruct((4 * RN[1], DIM), BF16)),
             in_specs=[vmem, any_space, any_space, any_space, any_space],
             out_specs=(any_space,) * 3,
             scratch_shapes=[
@@ -354,13 +391,17 @@
                 pltpu.VMEM((1, TOK), F32),
                 pltpu.VMEM((NDEV - 1, ROWS + 16, DIM), BF16),
                 pltpu.VMEM((NDEV, ROWS + 16, DIM), BF16),
-                pltpu.VMEM((NDEV - 1, ROWS, DIM), BF16),
+                pltpu.VMEM((ROWS, DIM), BF16),
+                pltpu.VMEM((6 * HALF, DIM), BF16),
+                pltpu.VMEM((6 * RN[0] + 2 * RN[1], DIM), BF16),
+                pltpu.VMEM((4 * RN[1], DIM), BF16),
                 pltpu.VMEM((2, DIM, HID), BF16),
                 pltpu.VMEM((2, HID, DIM), BF16),
                 pltpu.VMEM((4, BLK, DIM), BF16),
                 pltpu.VMEM((BLK, TOK), BF16),
                 pltpu.VMEM((TOK, 128), F32),
                 pltpu.VMEM((DIM, NEXP), F32),
+                pltpu.VMEM((DIM, 3 * NEXP), BF16),
                 dma, dma, dma((NBLK,)), dma, dma, dma((2,)), dma((2,)),
                 dma((NDEV - 1, 4)), dma((NDEV - 1, 4)), dma((NDEV - 1, 4)), dma((NDEV - 1, 4)),
             ],
@@ -376,7 +417,7 @@
             scratch_shapes=[
                 pltpu.VMEM((TOK, DIM), BF16),
                 pltpu.VMEM((TOK, 128), F32),
-                pltpu.VMEM((4, RN[1], DIM), BF16),
+                pltpu.VMEM((4 * RN[1], DIM), BF16),
                 pltpu.VMEM((TOK, DIM), BF16),
                 dma((NBLK,)), dma, dma, dma((NBLK,)),
             ],

time: 199 us -> 194 us (0.975)
  Pallas kernels: 199 us -> 194 us
    pallas_call x1, Pallas kernels: 13.5 us -> 10.4 us  [local_block(): pl.pallas_call(_finish, out_shape=jax.ShapeDtypeStruct((TOK, DIM), BF16),...]
where the time goes in v5:
time: 194 us
  Pallas kernels  194 us (100%)
    pallas_call x1, Pallas kernels, local_block(): pl.pallas_call(_kernel, out_shape=(jax.ShapeDtypeStruct((TOK, DIM), BF16)...  183 us
    pallas_call x1, Pallas kernels, local_block(): pl.pallas_call(_finish, out_shape=jax.ShapeDtypeStruct((TOK, DIM), BF16),...  10.4 us

profile of v5, /device:TPU:0, one launch (start us, length us, event | category | flops | bytes accessed | tf_op | source)
XLA Modules:
  0.0 193.7 jit_solution(4473791272287464486)
XLA Ops:
  0.0 183.3 %moe_step.1 = (bf16[3072,1024]{1,0:T(8,128)(2,1)}, f32[3072,128]{1,0:T(8,128)}, bf16[512,1024]{1,0:T(8,128)(2,1)}) custom-call(s32[1,3072]{1,0:T(1,128)} %bitcast.1, f32[1024,128]{1,0:T(8,128)} %wr_hbm.1, bf16[3072,1024]{1,0:T(8,128)(2,1)} %tok_hbm.1, bf16[16,1024,2816]{2,1,0:T(8,128)(2,1)} %win_hbm.1, bf16[16,2816,1024]{2,1,0:T(8,128)(2,1)} %wout_hbm.1), custom_call_target="tpu_custom_call" | custom-call | tf_op jit(solution)/shard_map/moe_step/pallas_call | solution.py:382
  183.3 10.4 %moe_finish.1 = bf16[3072,1024]{1,0:T(8,128)(2,1)} custom-call(bf16[3072,1024]{1,0:T(8,128)(2,1)} %get-tuple-element.8.y_hbm, f32[3072,128]{1,0:T(8,128)} %get-tuple-element.9.meta_hbm, bf16[512,1024]{1,0:T(8,128)(2,1)} %get-tuple-element.10.last_hbm), custom_call_target="tpu_custom_call" | custom-call | tf_op jit(solution)/shard_map/moe_finish/pallas_call | solution.py:412

commit v6 on v5

--- a/solution.py
+++ b/solution.py
@@ -165,7 +165,7 @@
                 d_copy(first, 0, 0).start()
             d_copy(second, 0, 0).start()
 
-        @pl.when(i == 10)
+        @pl.when(i == 9)
         def _():
             for k in order:
                 d_copy(k, 0, 1).start()
@@ -241,22 +241,22 @@
                 win_copy(e + 2).start()
                 wout_copy(e + 2).start()
 
-            @pl.when(e == 1)
+            @pl.when(e == 0)
             def _():
                 for k in order:
                     d_copy(k, 1, 0).start()
 
-            @pl.when(e == 7)
+            @pl.when(e == 5)
             def _():
                 for k in order:
                     d_copy(k, 1, 1).start()
 
-            @pl.when(e == 10)
+            @pl.when(e == 9)
             def _():
                 for k in far:
                     r_copy(k, 0, 0).start()
 
-            @pl.when(e == 14)
+            @pl.when(e == 13)
             def _():
                 for k in far:
                     r_copy(k, 0, 1).start()
@@ -285,7 +285,7 @@
         at = pl.ds(pl.multiple_of(b * BLK, BLK), BLK)
         return pltpu.make_async_copy(tok.at[at], y_hbm.at[at], y_sem.at[b])
 
-    def combine(sources, first=False, last=False):
+    def combine(sources, first=False, last=False, midway=None):
         sources = [(_targets(me, pieces), rows) for pieces, rows in sources]
 
         def block(b, _):
@@ -293,6 +293,8 @@
                 @pl.when(b >= 1)
                 def _():
                     y_copy(b - 1).start()
+            if midway:
+                pl.when(b == 4)(midway)
             at = pl.ds(pl.multiple_of(b * BLK, BLK), BLK)
             total = _pick(meta[at, 0:1], sources)
             if not first:
@@ -300,7 +302,7 @@
             tok[at, :] = total.astype(BF16)
             return 0
 
-        lax.fori_loop(0, NBLK, block, 0)
+        lax.fori_loop(0, NBLK, block, 0, unroll=2)
 
     def arrived(peers, *chunks):
         for h, j in chunks:
@@ -317,9 +319,12 @@
     arrived(far, (0, 1))
     for k in (6, 7):
         r_copy(k, 1, 1).start()
-    combine([([(k, 0, HALF) for k in range(2, 8)], ret_a)])
-    for k in (2, 4, 3, 5):
-        r_copy(k, 1, 1).start()
+
+    def send_last():
+        for k in (2, 4, 3, 5):
+            r_copy(k, 1, 1).start()
+
+    combine([([(k, 0, HALF) for k in range(2, 8)], ret_a)], midway=send_last)
     arrived(far, (1, 0))
     arrived((6, 7), (1, 1))
     combine([([(k, HALF, RN[0]) for k in range(2, 8)] + [(k, LAST, RN[1]) for k in (6, 7)], ret_b)], last=True)
@@ -369,7 +374,7 @@
         out_copy(b).start()
         return 0
 
-    lax.fori_loop(0, NBLK, block, 0)
+    lax.fori_loop(0, NBLK, block, 0, unroll=2)
     for b in range(NBLK):
         out_copy(b).wait()
 

time: 194 us -> 192 us (0.990)
  Pallas kernels: 194 us -> 192 us
where the time goes in v6:
time: 192 us
  Pallas kernels  192 us (100%)
    pallas_call x1, Pallas kernels, local_block(): pl.pallas_call(_kernel, out_shape=(jax.ShapeDtypeStruct((TOK, DIM), BF16)...  181 us
    pallas_call x1, Pallas kernels, local_block(): pl.pallas_call(_finish, out_shape=jax.ShapeDtypeStruct((TOK, DIM), BF16),...  10.3 us

profile of v6, /device:TPU:0, one launch (start us, length us, event | category | flops | bytes accessed | tf_op | source)
XLA Modules:
  0.0 191.8 jit_solution(3030381062241386028)
XLA Ops:
  0.0 181.4 %moe_step.1 = (bf16[3072,1024]{1,0:T(8,128)(2,1)}, f32[3072,128]{1,0:T(8,128)}, bf16[512,1024]{1,0:T(8,128)(2,1)}) custom-call(s32[1,3072]{1,0:T(1,128)} %bitcast.1, f32[1024,128]{1,0:T(8,128)} %wr_hbm.1, bf16[3072,1024]{1,0:T(8,128)(2,1)} %tok_hbm.1, bf16[16,1024,2816]{2,1,0:T(8,128)(2,1)} %win_hbm.1, bf16[16,2816,1024]{2,1,0:T(8,128)(2,1)} %wout_hbm.1), custom_call_target="tpu_custom_call" | custom-call | tf_op jit(solution)/shard_map/moe_step/pallas_call | solution.py:387
  181.4 10.3 %moe_finish.1 = bf16[3072,1024]{1,0:T(8,128)(2,1)} custom-call(bf16[3072,1024]{1,0:T(8,128)(2,1)} %get-tuple-element.8.y_hbm, f32[3072,128]{1,0:T(8,128)} %get-tuple-element.9.meta_hbm, bf16[512,1024]{1,0:T(8,128)(2,1)} %get-tuple-element.10.last_hbm), custom_call_target="tpu_custom_call" | custom-call | tf_op jit(solution)/shard_map/moe_finish/pallas_call | solution.py:417

commit v7 on v6

--- a/solution.py
+++ b/solution.py
@@ -60,8 +60,8 @@
 
 
 def _kernel(idx_ref, wr_hbm, tok_hbm, win_hbm, wout_hbm, y_hbm, meta_hbm, last_hbm,
-            tok, key, send, recv, ret_p, ret_a, ret_b, ret_c, win, wout, lhs, hid, meta, wr_ref, wr3,
-            wr_sem, tok_sem, y_sem, meta_sem, last_sem, win_sem, wout_sem,
+            tok, key, send, recv, ret_p, ret_a0, ret_a1, ret_b0, ret_b1, win, wout, lhs, hid, meta, wr_ref, wr3,
+            wr_sem, tok_sem, y_sem, meta_sem, win_sem, wout_sem,
             ds_sem, dr_sem, rs_sem, rr_sem):
     me = lax.axis_index("ep")
 
@@ -112,13 +112,14 @@
     def landing(k, h, j):
         if k == 1:
             return ret_p.at[pl.ds(pl.multiple_of(h * HALF + R0[j], 16), RN[j])]
+        at = pl.ds((k - 2) * RN[j], RN[j])
         if h == 0:
-            return ret_a.at[pl.ds((k - 2) * HALF + R0[j], RN[j])]
+            return (ret_a0, ret_a1)[j].at[at]
         if j == 0:
-            return ret_b.at[pl.ds((k - 2) * RN[0], RN[0])]
+            return ret_b0.at[at]
         if k >= 6:
-            return ret_b.at[pl.ds(6 * RN[0] + (k - 6) * RN[1], RN[1])]
-        return ret_c.at[pl.ds((k - 2) * RN[1], RN[1])]
+            return ret_b1.at[pl.ds((k - 6) * RN[1], RN[1])]
+        return last_hbm.at[at]
 
     def r_copy(k, h, j):
         rows = pl.ds(pl.multiple_of(h * HALF + R0[j], 16), RN[j])
@@ -241,12 +242,12 @@
                 win_copy(e + 2).start()
                 wout_copy(e + 2).start()
 
-            @pl.when(e == 0)
+            @pl.when(e == 1)
             def _():
                 for k in order:
                     d_copy(k, 1, 0).start()
 
-            @pl.when(e == 5)
+            @pl.when(e == 6)
             def _():
                 for k in order:
                     d_copy(k, 1, 1).start()
@@ -256,7 +257,7 @@
                 for k in far:
                     r_copy(k, 0, 0).start()
 
-            @pl.when(e == 13)
+            @pl.when(e == 15)
             def _():
                 for k in far:
                     r_copy(k, 0, 1).start()
@@ -294,7 +295,7 @@
                 def _():
                     y_copy(b - 1).start()
             if midway:
-                pl.when(b == 4)(midway)
+                pl.when(b == 8)(midway)
             at = pl.ds(pl.multiple_of(b * BLK, BLK), BLK)
             total = _pick(meta[at, 0:1], sources)
             if not first:
@@ -313,25 +314,24 @@
     meta_copy.start()
     arrived((1,), (0, 0), (0, 1), (1, 0), (1, 1))
     combine([([(0, 0, ROWS)], recv.at[0, :ROWS]), ([(1, 0, ROWS)], ret_p)], first=True)
+
+    def start(peers, h, j):
+        def go():
+            for k in peers:
+                r_copy(k, h, j).start()
+        return go
+
     arrived(far, (0, 0))
-    for k in far:
-        r_copy(k, 1, 0).start()
+    combine([([(k, R0[0], RN[0]) for k in range(2, 8)], ret_a0)], midway=start(far, 1, 0))
     arrived(far, (0, 1))
-    for k in (6, 7):
-        r_copy(k, 1, 1).start()
-
-    def send_last():
-        for k in (2, 4, 3, 5):
-            r_copy(k, 1, 1).start()
-
-    combine([([(k, 0, HALF) for k in range(2, 8)], ret_a)], midway=send_last)
+    combine([([(k, R0[1], RN[1]) for k in range(2, 8)], ret_a1)], midway=start((6, 7), 1, 1))
     arrived(far, (1, 0))
+    start((2, 4, 3, 5), 1, 1)()
+    combine([([(k, HALF, RN[0]) for k in range(2, 8)], ret_b0)])
     arrived((6, 7), (1, 1))
-    combine([([(k, HALF, RN[0]) for k in range(2, 8)] + [(k, LAST, RN[1]) for k in (6, 7)], ret_b)], last=True)
+    combine([([(k, LAST, RN[1]) for k in (6, 7)], ret_b1)], last=True)
+    y_copy(NBLK - 1).start()
     arrived((2, 3, 4, 5), (1, 1))
-    y_copy(NBLK - 1).start()
-    last_copy = pltpu.make_async_copy(ret_c, last_hbm, last_sem)
-    last_copy.start()
 
     for h in range(2):
         for j in range(2):
@@ -341,7 +341,6 @@
     for b in range(NBLK):
         y_copy(b).wait()
     meta_copy.wait()
-    last_copy.wait()
 
 
 def _finish(y_hbm, meta_hbm, last_hbm, out_hbm, y, meta, last, out, y_sem, meta_sem, last_sem, out_sem):
@@ -356,17 +355,23 @@
     def out_copy(b):
         return pltpu.make_async_copy(out.at[rows(b)], out_hbm.at[rows(b)], out_sem.at[b])
 
+    def meta_copy(b):
+        return pltpu.make_async_copy(meta_hbm.at[rows(b)], meta.at[rows(b)], meta_sem.at[b])
+
     last_copy = pltpu.make_async_copy(last_hbm, last, last_sem)
-    meta_copy = pltpu.make_async_copy(meta_hbm, meta, meta_sem)
     last_copy.start()
-    meta_copy.start()
-    for b in range(NBLK):
+    for b in range(3):
+        meta_copy(b).start()
         y_copy(b).start()
     target = _targets(me, [(k, LAST, RN[1]) for k in range(2, 6)])
     last_copy.wait()
-    meta_copy.wait()
 
     def block(b, _):
+        @pl.when(b + 3 < NBLK)
+        def _():
+            meta_copy(b + 3).start()
+            y_copy(b + 3).start()
+        meta_copy(b).wait()
         y_copy(b).wait()
         total = _pick(meta[rows(b), 0:1], [(target, last)])
         total = total + y[rows(b), :].astype(F32)
@@ -374,7 +379,7 @@
         out_copy(b).start()
         return 0
 
-    lax.fori_loop(0, NBLK, block, 0, unroll=2)
+    lax.fori_loop(0, NBLK, block, 0)
     for b in range(NBLK):
         out_copy(b).wait()
 
@@ -397,9 +402,10 @@
                 pltpu.VMEM((NDEV - 1, ROWS + 16, DIM), BF16),
                 pltpu.VMEM((NDEV, ROWS + 16, DIM), BF16),
                 pltpu.VMEM((ROWS, DIM), BF16),
-                pltpu.VMEM((6 * HALF, DIM), BF16),
-                pltpu.VMEM((6 * RN[0] + 2 * RN[1], DIM), BF16),
-                pltpu.VMEM((4 * RN[1], DIM), BF16),
+                pltpu.VMEM((6 * RN[0], DIM), BF16),
+                pltpu.VMEM((6 * RN[1], DIM), BF16),
+                pltpu.VMEM((6 * RN[0], DIM), BF16),
+                pltpu.VMEM((2 * RN[1], DIM), BF16),
                 pltpu.VMEM((2, DIM, HID), BF16),
                 pltpu.VMEM((2, HID, DIM), BF16),
                 pltpu.VMEM((4, BLK, DIM), BF16),
@@ -407,7 +413,7 @@
                 pltpu.VMEM((TOK, 128), F32),
                 pltpu.VMEM((DIM, NEXP), F32),
                 pltpu.VMEM((DIM, 3 * NEXP), BF16),
-                dma, dma, dma((NBLK,)), dma, dma, dma((2,)), dma((2,)),
+                dma, dma, dma((NBLK,)), dma, dma((2,)), dma((2,)),
                 dma((NDEV - 1, 4)), dma((NDEV - 1, 4)), dma((NDEV - 1, 4)), dma((NDEV - 1, 4)),
             ],
             compiler_params=pltpu.CompilerParams(
@@ -424,7 +430,7 @@
                 pltpu.VMEM((TOK, 128), F32),
                 pltpu.VMEM((4 * RN[1], DIM), BF16),
                 pltpu.VMEM((TOK, DIM), BF16),
-                dma((NBLK,)), dma, dma, dma((NBLK,)),
+                dma((NBLK,)), dma((NBLK,)), dma, dma((NBLK,)),
             ],
             compiler_params=pltpu.CompilerParams(vmem_limit_bytes=60 * 2**20),
             name="moe_finish",

time: 192 us -> 189 us (0.984)
  Pallas kernels: 192 us -> 189 us
where the time goes in v7:
time: 189 us
  Pallas kernels  189 us (100%)
    pallas_call x1, Pallas kernels, local_block(): pl.pallas_call(_kernel, out_shape=(jax.ShapeDtypeStruct((TOK, DIM), BF16)...  181 us
    pallas_call x1, Pallas kernels, local_block(): pl.pallas_call(_finish, out_shape=jax.ShapeDtypeStruct((TOK, DIM), BF16),...  8.74 us

profile of v7, /device:TPU:0, one launch (start us, length us, event | category | flops | bytes accessed | tf_op | source)
XLA Modules:
  0.0 189.3 jit_solution(12779317211458777727)
XLA Ops:
  0.0 180.5 %moe_step.1 = (bf16[3072,1024]{1,0:T(8,128)(2,1)}, f32[3072,128]{1,0:T(8,128)}, bf16[512,1024]{1,0:T(8,128)(2,1)}) custom-call(s32[1,3072]{1,0:T(1,128)} %bitcast.1, f32[1024,128]{1,0:T(8,128)} %wr_hbm.1, bf16[3072,1024]{1,0:T(8,128)(2,1)} %tok_hbm.1, bf16[16,1024,2816]{2,1,0:T(8,128)(2,1)} %win_hbm.1, bf16[16,2816,1024]{2,1,0:T(8,128)(2,1)} %wout_hbm.1), custom_call_target="tpu_custom_call" | custom-call | tf_op jit(solution)/shard_map/moe_step/pallas_call | solution.py:392
  180.5 8.7 %moe_finish.1 = bf16[3072,1024]{1,0:T(8,128)(2,1)} custom-call(bf16[3072,1024]{1,0:T(8,128)(2,1)} %get-tuple-element.8.y_hbm, f32[3072,128]{1,0:T(8,128)} %get-tuple-element.9.meta_hbm, bf16[512,1024]{1,0:T(8,128)(2,1)} %get-tuple-element.10.last_hbm), custom_call_target="tpu_custom_call" | custom-call | tf_op jit(solution)/shard_map/moe_finish/pallas_call | solution.py:423

commit v8 on v7

--- a/solution.py
+++ b/solution.py
@@ -100,7 +100,6 @@
     for e in range(2):
         win_copy(e).start()
         wout_copy(e).start()
-    pl.semaphore_wait(barrier, NDEV - 1)
 
     def d_copy(k, h, j):
         rows = pl.ds(pl.multiple_of(h * HALF + D0[j], 16), DN[j])
@@ -159,6 +158,10 @@
                 recv[0, rows, cols] = part[:128]
 
             send[second - 1, rows, cols] = part[128:]
+        @pl.when(i == 0)
+        def _():
+            pl.semaphore_wait(barrier, NDEV - 1)
+
         @pl.when(i < 4)
         def _():
             @pl.when(p < 3)
@@ -379,7 +382,7 @@
         out_copy(b).start()
         return 0
 
-    lax.fori_loop(0, NBLK, block, 0)
+    lax.fori_loop(0, NBLK, block, 0, unroll=2)
     for b in range(NBLK):
         out_copy(b).wait()
 

time: 189 us -> 189 us (level)
  no operation moved by 1% of the time
where the time goes in v8:
time: 189 us
  Pallas kernels  189 us (100%)
    pallas_call x1, Pallas kernels, local_block(): pl.pallas_call(_kernel, out_shape=(jax.ShapeDtypeStruct((TOK, DIM), BF16)...  180 us
    pallas_call x1, Pallas kernels, local_block(): pl.pallas_call(_finish, out_shape=jax.ShapeDtypeStruct((TOK, DIM), BF16),...  8.67 us

profile of v8, /device:TPU:0, one launch (start us, length us, event | category | flops | bytes accessed | tf_op | source)
XLA Modules:
  0.0 188.6 jit_solution(2516251720647856116)
XLA Ops:
  0.0 179.9 %moe_step.1 = (bf16[3072,1024]{1,0:T(8,128)(2,1)}, f32[3072,128]{1,0:T(8,128)}, bf16[512,1024]{1,0:T(8,128)(2,1)}) custom-call(s32[1,3072]{1,0:T(1,128)} %bitcast.1, f32[1024,128]{1,0:T(8,128)} %wr_hbm.1, bf16[3072,1024]{1,0:T(8,128)(2,1)} %tok_hbm.1, bf16[16,1024,2816]{2,1,0:T(8,128)(2,1)} %win_hbm.1, bf16[16,2816,1024]{2,1,0:T(8,128)(2,1)} %wout_hbm.1), custom_call_target="tpu_custom_call" | custom-call | tf_op jit(solution)/shard_map/moe_step/pallas_call | solution.py:395
  179.9 8.7 %moe_finish.1 = bf16[3072,1024]{1,0:T(8,128)(2,1)} custom-call(bf16[3072,1024]{1,0:T(8,128)(2,1)} %get-tuple-element.8.y_hbm, f32[3072,128]{1,0:T(8,128)} %get-tuple-element.9.meta_hbm, bf16[512,1024]{1,0:T(8,128)(2,1)} %get-tuple-element.10.last_hbm), custom_call_target="tpu_custom_call" | custom-call | tf_op jit(solution)/shard_map/moe_finish/pallas_call | solution.py:426

commit v9 on v8

--- a/solution.py
+++ b/solution.py
@@ -289,7 +289,7 @@
         at = pl.ds(pl.multiple_of(b * BLK, BLK), BLK)
         return pltpu.make_async_copy(tok.at[at], y_hbm.at[at], y_sem.at[b])
 
-    def combine(sources, first=False, last=False, midway=None):
+    def combine(sources, first=False, last=False, midway=None, when=0):
         sources = [(_targets(me, pieces), rows) for pieces, rows in sources]
 
         def block(b, _):
@@ -298,7 +298,7 @@
                 def _():
                     y_copy(b - 1).start()
             if midway:
-                pl.when(b == 8)(midway)
+                pl.when(b == when)(midway)
             at = pl.ds(pl.multiple_of(b * BLK, BLK), BLK)
             total = _pick(meta[at, 0:1], sources)
             if not first:
@@ -325,9 +325,9 @@
         return go
 
     arrived(far, (0, 0))
-    combine([([(k, R0[0], RN[0]) for k in range(2, 8)], ret_a0)], midway=start(far, 1, 0))
+    combine([([(k, R0[0], RN[0]) for k in range(2, 8)], ret_a0)], midway=start(far, 1, 0), when=11)
     arrived(far, (0, 1))
-    combine([([(k, R0[1], RN[1]) for k in range(2, 8)], ret_a1)], midway=start((6, 7), 1, 1))
+    combine([([(k, R0[1], RN[1]) for k in range(2, 8)], ret_a1)], midway=start((6, 7), 1, 1), when=2)
     arrived(far, (1, 0))
     start((2, 4, 3, 5), 1, 1)()
     combine([([(k, HALF, RN[0]) for k in range(2, 8)], ret_b0)])
@@ -363,17 +363,17 @@
 
     last_copy = pltpu.make_async_copy(last_hbm, last, last_sem)
     last_copy.start()
-    for b in range(3):
+    for b in range(5):
         meta_copy(b).start()
         y_copy(b).start()
     target = _targets(me, [(k, LAST, RN[1]) for k in range(2, 6)])
     last_copy.wait()
 
     def block(b, _):
-        @pl.when(b + 3 < NBLK)
+        @pl.when(b + 5 < NBLK)
         def _():
-            meta_copy(b + 3).start()
-            y_copy(b + 3).start()
+            meta_copy(b + 5).start()
+            y_copy(b + 5).start()
         meta_copy(b).wait()
         y_copy(b).wait()
         total = _pick(meta[rows(b), 0:1], [(target, last)])

time: 189 us -> 191 us (1.011)
  no operation moved by 1% of the time
where the time goes in v9:
time: 191 us; the launch traced here: 190 us
  Pallas kernels  190 us (99%)
    pallas_call x1, Pallas kernels, local_block(): pl.pallas_call(_kernel, out_shape=(jax.ShapeDtypeStruct((TOK, DIM), BF16)...  181 us
    pallas_call x1, Pallas kernels, local_block(): pl.pallas_call(_finish, out_shape=jax.ShapeDtypeStruct((TOK, DIM), BF16),...  9.05 us

profile of v9, /device:TPU:0, one launch (start us, length us, event | category | flops | bytes accessed | tf_op | source)
XLA Modules:
  0.0 190.5 jit_solution(12918554654240118955)
XLA Ops:
  0.0 181.4 %moe_step.1 = (bf16[3072,1024]{1,0:T(8,128)(2,1)}, f32[3072,128]{1,0:T(8,128)}, bf16[512,1024]{1,0:T(8,128)(2,1)}) custom-call(s32[1,3072]{1,0:T(1,128)} %bitcast.1, f32[1024,128]{1,0:T(8,128)} %wr_hbm.1, bf16[3072,1024]{1,0:T(8,128)(2,1)} %tok_hbm.1, bf16[16,1024,2816]{2,1,0:T(8,128)(2,1)} %win_hbm.1, bf16[16,2816,1024]{2,1,0:T(8,128)(2,1)} %wout_hbm.1), custom_call_target="tpu_custom_call" | custom-call | tf_op jit(solution)/shard_map/moe_step/pallas_call | solution.py:395
  181.4 9.1 %moe_finish.1 = bf16[3072,1024]{1,0:T(8,128)(2,1)} custom-call(bf16[3072,1024]{1,0:T(8,128)(2,1)} %get-tuple-element.8.y_hbm, f32[3072,128]{1,0:T(8,128)} %get-tuple-element.9.meta_hbm, bf16[512,1024]{1,0:T(8,128)(2,1)} %get-tuple-element.10.last_hbm), custom_call_target="tpu_custom_call" | custom-call | tf_op jit(solution)/shard_map/moe_finish/pallas_call | solution.py:426

commit v10 on v9

--- a/solution.py
+++ b/solution.py
@@ -325,9 +325,9 @@
         return go
 
     arrived(far, (0, 0))
-    combine([([(k, R0[0], RN[0]) for k in range(2, 8)], ret_a0)], midway=start(far, 1, 0), when=11)
+    combine([([(k, R0[0], RN[0]) for k in range(2, 8)], ret_a0)], midway=start(far, 1, 0), when=4)
     arrived(far, (0, 1))
-    combine([([(k, R0[1], RN[1]) for k in range(2, 8)], ret_a1)], midway=start((6, 7), 1, 1), when=2)
+    combine([([(k, R0[1], RN[1]) for k in range(2, 8)], ret_a1)], midway=start((6, 7), 1, 1), when=8)
     arrived(far, (1, 0))
     start((2, 4, 3, 5), 1, 1)()
     combine([([(k, HALF, RN[0]) for k in range(2, 8)], ret_b0)])
@@ -363,17 +363,17 @@
 
     last_copy = pltpu.make_async_copy(last_hbm, last, last_sem)
     last_copy.start()
-    for b in range(5):
+    for b in range(2):
         meta_copy(b).start()
         y_copy(b).start()
     target = _targets(me, [(k, LAST, RN[1]) for k in range(2, 6)])
     last_copy.wait()
 
     def block(b, _):
-        @pl.when(b + 5 < NBLK)
+        @pl.when(b + 2 < NBLK)
         def _():
-            meta_copy(b + 5).start()
-            y_copy(b + 5).start()
+            meta_copy(b + 2).start()
+            y_copy(b + 2).start()
         meta_copy(b).wait()
         y_copy(b).wait()
         total = _pick(meta[rows(b), 0:1], [(target, last)])

time: 191 us -> 189 us (0.990)
  Pallas kernels: 190 us -> 188 us
    pallas_call x1, Pallas kernels: 181 us -> 179 us  [local_block(): pl.pallas_call(_kernel, out_shape=(jax.ShapeDtypeStruct((TOK, DIM), BF16)...]
where the time goes in v10:
time: 189 us; the launch traced here: 188 us
  Pallas kernels  188 us (99%)
    pallas_call x1, Pallas kernels, local_block(): pl.pallas_call(_kernel, out_shape=(jax.ShapeDtypeStruct((TOK, DIM), BF16)...  179 us
    pallas_call x1, Pallas kernels, local_block(): pl.pallas_call(_finish, out_shape=jax.ShapeDtypeStruct((TOK, DIM), BF16),...  9.52 us

profile of v10, /device:TPU:0, one launch (start us, length us, event | category | flops | bytes accessed | tf_op | source)
XLA Modules:
  0.0 188.4 jit_solution(2448246838877074070)
XLA Ops:
  0.0 178.9 %moe_step.1 = (bf16[3072,1024]{1,0:T(8,128)(2,1)}, f32[3072,128]{1,0:T(8,128)}, bf16[512,1024]{1,0:T(8,128)(2,1)}) custom-call(s32[1,3072]{1,0:T(1,128)} %bitcast.1, f32[1024,128]{1,0:T(8,128)} %wr_hbm.1, bf16[3072,1024]{1,0:T(8,128)(2,1)} %tok_hbm.1, bf16[16,1024,2816]{2,1,0:T(8,128)(2,1)} %win_hbm.1, bf16[16,2816,1024]{2,1,0:T(8,128)(2,1)} %wout_hbm.1), custom_call_target="tpu_custom_call" | custom-call | tf_op jit(solution)/shard_map/moe_step/pallas_call | solution.py:395
  178.9 9.5 %moe_finish.1 = bf16[3072,1024]{1,0:T(8,128)(2,1)} custom-call(bf16[3072,1024]{1,0:T(8,128)(2,1)} %get-tuple-element.8.y_hbm, f32[3072,128]{1,0:T(8,128)} %get-tuple-element.9.meta_hbm, bf16[512,1024]{1,0:T(8,128)(2,1)} %get-tuple-element.10.last_hbm), custom_call_target="tpu_custom_call" | custom-call | tf_op jit(solution)/shard_map/moe_finish/pallas_call | solution.py:426
